TPU v7x, 32 devices: a 4x4x1 block of a 4x4x8 slice. The times are simulated.
32 devices in a mesh: dp: 1 (over z), col: 4 (over y), row: 8 (over x, core).
Axes of the slice: x: 4, y: 4, z: 1, core: 2. Of those that a mesh axis runs over, the one named last changes fastest.
The devices are a block of a 4x4x8 slice.
Arguments:
- latent: bfloat16 [2, 32, 192, 1280], P('dp', 'row', 'col')
- t_emb: bfloat16 [2, 1280], P('dp')
- res_norm: bfloat16 [2, 2, 2, 1280], replicated
- res_conv: bfloat16 [2, 2, 3, 3, 1280, 1280], replicated
- res_temb: bfloat16 [2, 1280, 1280], replicated
- attn_norm: bfloat16 [2, 1280], replicated
- attn_proj: bfloat16 [4, 20, 1280, 64], replicated
Outputs:
- output: bfloat16 [2, 32, 192, 1280], P('dp', 'row', 'col')
All inputs are finite; a program needn't handle non-finite values.
Results may differ from a plain program's by a relative error of at most 0.0117124.
Values are sent between devices in bfloat16 or wider.
A program may use at most 768 MiB of HBM per device.

v0:
```python
import jax
import jax.numpy as jnp
from jax import lax
from jax.sharding import PartitionSpec as P

GROUPS = 32
EPS = 1e-5


def group_norm(values, gn_scale, gn_shift, n_dev):
    n_batch, n_rows, n_cols, n_chan = values.shape
    group_ch = n_chan // GROUPS
    grouped = values.astype(jnp.float32).reshape(n_batch, n_rows, n_cols, GROUPS, group_ch)
    part_sums = jnp.stack([jnp.sum(grouped, axis=(1, 2, 4)), jnp.sum(grouped * grouped, axis=(1, 2, 4))])
    moments = lax.psum(part_sums, ('row', 'col')) / (n_rows * n_cols * group_ch * n_dev)
    mean_val = moments[0]
    inv_std = lax.rsqrt(moments[1] - mean_val * mean_val + EPS)
    normed = (grouped - mean_val[:, None, None, :, None]) * inv_std[:, None, None, :, None]
    return normed.reshape(values.shape) * gn_scale.astype(jnp.float32) + gn_shift.astype(jnp.float32)


def halo_conv(acts_in, kernel, n_row, n_col):
    to_next_row = [(i, i + 1) for i in range(n_row - 1)]
    to_prev_row = [(i + 1, i) for i in range(n_row - 1)]
    to_next_col = [(i, i + 1) for i in range(n_col - 1)]
    to_prev_col = [(i + 1, i) for i in range(n_col - 1)]
    from_above = lax.ppermute(acts_in[:, -1:], 'row', to_next_row)
    from_below = lax.ppermute(acts_in[:, :1], 'row', to_prev_row)
    row_padded = jnp.concatenate([from_above, acts_in, from_below], axis=1)
    from_left = lax.ppermute(row_padded[:, :, -1:], 'col', to_next_col)
    from_right = lax.ppermute(row_padded[:, :, :1], 'col', to_prev_col)
    padded = jnp.concatenate([from_left, row_padded, from_right], axis=2)
    return lax.conv_general_dilated(padded, kernel, (1, 1), 'VALID', dimension_numbers=('NHWC', 'HWIO', 'NHWC'), preferred_element_type=jnp.float32)


def res_block(latent, t_emb, norm_par, kernels, w_temb, n_row, n_col):
    n_dev = n_row * n_col
    t_act = jax.nn.silu(t_emb.astype(jnp.float32)).astype(jnp.bfloat16)
    t_proj = jnp.dot(t_act, w_temb, preferred_element_type=jnp.float32)
    first_act = jax.nn.silu(group_norm(latent, norm_par[0, 0], norm_par[0, 1], n_dev)).astype(jnp.bfloat16)
    hidden = (halo_conv(first_act, kernels[0], n_row, n_col) + t_proj[:, None, None, :]).astype(jnp.bfloat16)
    second_act = jax.nn.silu(group_norm(hidden, norm_par[1, 0], norm_par[1, 1], n_dev)).astype(jnp.bfloat16)
    return (latent.astype(jnp.float32) + halo_conv(second_act, kernels[1], n_row, n_col)).astype(jnp.bfloat16)


def attend(queries, keys_all, values_all, n_blocks):
    n_batch, n_query, n_heads, head_dim = queries.shape
    blk_len = keys_all.shape[1] // n_blocks
    key_blocks = keys_all.reshape(n_batch, n_blocks, blk_len, n_heads, head_dim)
    val_blocks = values_all.reshape(n_batch, n_blocks, blk_len, n_heads, head_dim)
    inv_scale = head_dim ** -0.5

    def key_step(blk_idx, loop_state):
        run_max, run_sum, out_acc = loop_state
        key_blk = lax.dynamic_index_in_dim(key_blocks, blk_idx, axis=1, keepdims=False)
        val_blk = lax.dynamic_index_in_dim(val_blocks, blk_idx, axis=1, keepdims=False)
        logits = jnp.einsum('bqhd,bkhd->bhqk', queries, key_blk, preferred_element_type=jnp.float32) * inv_scale
        new_max = jnp.maximum(run_max, jnp.max(logits, axis=-1))
        rescale = jnp.exp(run_max - new_max)
        exp_logits = jnp.exp(logits - new_max[..., None])
        run_sum = run_sum * rescale + jnp.sum(exp_logits, axis=-1)
        out_acc = out_acc * rescale[..., None] + jnp.einsum('bhqk,bkhd->bhqd', exp_logits.astype(jnp.bfloat16), val_blk, preferred_element_type=jnp.float32)
        return new_max, run_sum, out_acc

    carry_init = (jnp.full((n_batch, n_heads, n_query), -jnp.inf, jnp.float32), jnp.zeros((n_batch, n_heads, n_query), jnp.float32), jnp.zeros((n_batch, n_heads, n_query, head_dim), jnp.float32))
    run_max, run_sum, out_acc = lax.fori_loop(0, n_blocks, key_step, carry_init)
    return out_acc / run_sum[..., None]


def attn_block(latent, norm_par, proj_w, n_dev):
    n_batch, n_rows, n_cols, n_chan = latent.shape
    normed = group_norm(latent, norm_par[0], norm_par[1], n_dev).astype(jnp.bfloat16).reshape(n_batch, n_rows * n_cols, n_chan)
    qkv_loc = jnp.einsum('bnc,khcd->kbnhd', normed, proj_w[:3], preferred_element_type=jnp.float32).astype(jnp.bfloat16)
    kv_all = lax.all_gather(qkv_loc[1:], ('row', 'col'), axis=2, tiled=True)
    attn_out = attend(qkv_loc[0], kv_all[0], kv_all[1], n_dev).astype(jnp.bfloat16)
    out_proj = jnp.einsum('bhqd,hcd->bqc', attn_out, proj_w[3], preferred_element_type=jnp.float32)
    return (latent.astype(jnp.float32) + out_proj.reshape(latent.shape)).astype(jnp.bfloat16)


def solution(mesh):
    n_row = mesh.shape['row']
    n_col = mesh.shape['col']

    def run_stage(latent, t_emb, res_norm, res_conv, res_temb, attn_norm, attn_proj):
        hidden = res_block(latent, t_emb, res_norm[0], res_conv[0], res_temb[0], n_row, n_col)
        hidden = attn_block(hidden, attn_norm, attn_proj, n_row * n_col)
        return res_block(hidden, t_emb, res_norm[1], res_conv[1], res_temb[1], n_row, n_col)

    spec_x = P('dp', 'row', 'col', None)
    return jax.shard_map(run_stage, mesh=mesh, in_specs=(spec_x, P('dp', None), P(), P(), P(), P(), P()), out_specs=spec_x, check_vma=False)
```

profile of v0, /device:TPU:97, one launch (start us, length us, event | category | flops | bytes accessed | tf_op | source)
XLA Modules:
  0.0 1676.1 jit_solution(5754037547567896618)
XLA Ops:
  8.4 49.8 %psum.35 = f32[2,2,32]{2,1,0:T(2,128)S(1)} all-reduce(f32[2,2,32]{2,1,0:T(2,128)S(1)} %pad_maximum_fusion.12), channel_id=1, replica_groups=mesh['dp'=1,'col'=4,'row'=8] {'row','col'}, use_global_device_ids=true, to_apply=%region_4.5 | all-reduce | flops 128 | bytes 1024 | tf_op jit(solution)/shard_map/psum | solution.py:15
  87.4 23.9 %fusion.164 = (f32[4,16,7,1280]{3,1,2,0:T(8,128)}, f32[4,16,7,1280]{3,1,2,0:T(8,128)S(1)}) fusion(f32[4,16,7,1280]{3,0,2,1:T(4,128)} %bitcast.281, bf16[2,2,3,3,1280,1280]{5,4,3,2,1,0:T(8,128)(2,1)} %param.12, bf16[6,2,8,9,1280]{4,1,3,2,0:T(2,128)(2,1)} %fusion.91, pred[16,7]{0,1:T(8,128)(4,1)S(1)} %copy-done.12), kind=kOutput, calls=%fused_computation.220 | convolution fusion | flops 13214924800 | bytes 38584432 | tf_op jit(solution)/shard_map/conv_general_dilated | solution.py:33
  116.7 45.3 %psum.36 = f32[2,2,32]{2,1,0:T(2,128)S(1)} all-reduce(f32[2,2,32]{2,1,0:T(2,128)S(1)} %pad_maximum_fusion.13), channel_id=1, replica_groups=mesh['dp'=1,'col'=4,'row'=8] {'row','col'}, use_global_device_ids=true, to_apply=%region_9.10 | all-reduce | flops 128 | bytes 1024 | tf_op jit(solution)/shard_map/psum | solution.py:15
  189.8 17.0 %fusion.50 = f32[4,16,7,1280]{3,1,2,0:T(8,128)S(1)} fusion(bf16[2,2,3,3,1280,1280]{5,4,3,2,1,0:T(8,128)(2,1)} %param.12, bf16[6,2,8,9,1280]{4,1,3,2,0:T(2,128)(2,1)S(1)} %fusion.92, pred[16,7]{0,1:T(8,128)(4,1)S(1)} %copy-done.12), kind=kOutput, calls=%fused_computation.66 | convolution fusion | flops 13212631040 | bytes 33996912 | tf_op jit(solution)/shard_map/conv_general_dilated | solution.py:33
  210.3 45.9 %psum.37 = f32[2,2,32]{2,1,0:T(2,128)S(1)} all-reduce(f32[2,2,32]{2,1,0:T(2,128)S(1)} %pad_maximum_fusion.14), channel_id=1, replica_groups=mesh['dp'=1,'col'=4,'row'=8] {'row','col'}, use_global_device_ids=true, to_apply=%region_14.15 | all-reduce | flops 128 | bytes 1024 | tf_op jit(solution)/shard_map/psum | solution.py:15
  256.9 9.3 convert_bitcast_fusion
  268.3 7.1 copy.142
  278.0 344.3 %all-gather.2.cloned.1.call-done = bf16[2,2,6144,20,64]{4,1,3,0,2:T(2,128)(2,1)} async-done(((bf16[2,2,192,20,64]{4,1,3,0,2:T(2,128)(2,1)}), bf16[2,2,6144,20,64]{4,1,3,0,2:T(2,128)(2,1)}) %all-gather.2.cloned.1.call-update) | async-done | bytes 62914576 | tf_op jit(solution)/shard_map/all_gather | solution.py:74
  622.3 94.5 %fusion.159 = (bf16[1,2,6144,20,64]{4,1,3,0,2:T(2,128)(2,1)}, bf16[1,2,6144,20,64]{4,1,3,0,2:T(2,128)(2,1)}) fusion(bf16[2,2,6144,20,64]{4,1,3,0,2:T(2,128)(2,1)} %all-gather.2.cloned.1.call-done), kind=kLoop, calls=%fused_computation.215 | loop fusion | bytes 125829120 | tf_op jit(solution)/shard_map/slice | solution.py:75
  716.9 135.7 %copy.143 = bf16[2,32,192,20,64]{2,4,3,0,1:T(8,128)(2,1)} copy(bf16[2,32,192,20,64]{4,0,3,2,1:T(2,128)(2,1)} %bitcast.260) | data formatting | bytes 62914560
  852.6 135.7 %copy.144 = bf16[2,32,192,20,64]{2,4,3,0,1:T(8,128)(2,1)} copy(bf16[2,32,192,20,64]{4,0,3,2,1:T(2,128)(2,1)} %bitcast.259) | data formatting | bytes 62914560
  988.3 474.2 %while.18 = (s32[]{:T(128)}, f32[2,20,192]{2,1,0:T(8,128)S(1)}, f32[2,20,192]{2,1,0:T(8,128)S(1)}, f32[2,20,192,64]{2,3,1,0:T(8,128)S(1)}, bf16[2,32,192,20,64]{...) while((s32[]{:T(128)}, f32[2,20,192]{2,1,0:T(8,128)S(1)}, ...), condition=%wide.region_18.19_spmd.clone, body=%wide.region_15.18_spmd.clone.sunk | while | flops 390796800 | bytes 49644676 | solution.py:66
  988.3 6.1 bitcast_reduce_fusion.2
  1003.1 6.1 bitcast_reduce_fusion.2
  1017.9 6.1 bitcast_reduce_fusion.2
  1032.8 6.1 bitcast_reduce_fusion.2
  1047.6 6.1 bitcast_reduce_fusion.2
  1062.4 6.1 bitcast_reduce_fusion.2
  1077.2 6.1 bitcast_reduce_fusion.2
  1092.0 6.1 bitcast_reduce_fusion.2
  1106.9 6.1 bitcast_reduce_fusion.2
  1121.7 6.1 bitcast_reduce_fusion.2
  1136.5 6.1 bitcast_reduce_fusion.2
  1151.3 6.1 bitcast_reduce_fusion.2
  1166.1 6.1 bitcast_reduce_fusion.2
  1180.9 6.1 bitcast_reduce_fusion.2
  1195.8 6.1 bitcast_reduce_fusion.2
  1210.6 6.1 bitcast_reduce_fusion.2
  1225.4 6.1 bitcast_reduce_fusion.2
  1240.2 6.1 bitcast_reduce_fusion.2
  1255.0 6.1 bitcast_reduce_fusion.2
  1269.9 6.1 bitcast_reduce_fusion.2
  1284.7 6.1 bitcast_reduce_fusion.2
  1299.5 6.1 bitcast_reduce_fusion.2
  1314.3 6.1 bitcast_reduce_fusion.2
  1329.1 6.1 bitcast_reduce_fusion.2
  1344.0 6.1 bitcast_reduce_fusion.2
  1358.8 6.1 bitcast_reduce_fusion.2
  1373.6 6.1 bitcast_reduce_fusion.2
  1388.4 6.1 bitcast_reduce_fusion.2
  1403.2 6.1 bitcast_reduce_fusion.2
  1418.1 6.1 bitcast_reduce_fusion.2
  1432.9 6.1 bitcast_reduce_fusion.2
  1447.7 6.1 bitcast_reduce_fusion.2
  1472.7 44.7 %psum.38 = f32[2,2,32]{2,1,0:T(2,128)S(1)} all-reduce(f32[2,2,32]{2,1,0:T(2,128)S(1)} %pad_maximum_fusion.15), channel_id=1, replica_groups=mesh['dp'=1,'col'=4,'row'=8] {'row','col'}, use_global_device_ids=true, to_apply=%region_23.24 | all-reduce | flops 128 | bytes 1024 | tf_op jit(solution)/shard_map/psum | solution.py:15
  1544.7 23.7 %fusion.165 = (f32[4,16,7,1280]{3,1,2,0:T(8,128)}, f32[4,16,7,1280]{3,1,2,0:T(8,128)S(1)}) fusion(f32[4,16,7,1280]{3,0,2,1:T(4,128)} %bitcast.282, bf16[2,2,3,3,1280,1280]{5,4,3,2,1,0:T(8,128)(2,1)} %param.12, bf16[6,2,8,9,1280]{4,1,3,2,0:T(2,128)(2,1)} %fusion.93, pred[16,7]{0,1:T(8,128)(4,1)S(1)} %copy-done.13), kind=kOutput, calls=%fused_computation.221 | convolution fusion | flops 13214924800 | bytes 38584432 | tf_op jit(solution)/shard_map/conv_general_dilated | solution.py:33
  1573.8 45.4 %psum.39 = f32[2,2,32]{2,1,0:T(2,128)S(1)} all-reduce(f32[2,2,32]{2,1,0:T(2,128)S(1)} %pad_maximum_fusion.16), channel_id=1, replica_groups=mesh['dp'=1,'col'=4,'row'=8] {'row','col'}, use_global_device_ids=true, to_apply=%region_28.29 | all-reduce | flops 128 | bytes 1024 | tf_op jit(solution)/shard_map/psum | solution.py:15
  1648.2 17.7 %fusion.56 = f32[4,16,7,1280]{3,1,2,0:T(8,128)S(1)} fusion(bf16[2,2,3,3,1280,1280]{5,4,3,2,1,0:T(8,128)(2,1)} %param.12, bf16[6,2,8,9,1280]{4,1,3,2,0:T(2,128)(2,1)} %fusion.94, pred[16,7]{0,1:T(8,128)(4,1)S(1)} %copy-done.13), kind=kOutput, calls=%fused_computation.68 | convolution fusion | flops 13212631040 | bytes 33996912 | tf_op jit(solution)/shard_map/conv_general_dilated | solution.py:33
  (431 shorter events, 425.3 us)
Async XLA Ops:
  6.5 615.8 %all-gather.2.cloned.1.call-start = ((), (), s32[]{:S(2)}) async-start(), calls=%async_computation | async-start | bytes 129761280 | tf_op jit(solution)/shard_map/all_gather | solution.py:74
  60.0 15.3 copy-start.10
  62.0 5.1 collective-permute-start
  63.9 7.5 collective-permute-start.1
  71.6 6.2 collective-permute-start.2
  74.0 5.0 collective-permute-start.3
  165.3 10.2 collective-permute-start.5
  168.1 6.1 collective-permute-start.4
  171.1 8.5 copy-start.9
  175.5 4.2 collective-permute-start.6
  178.3 4.8 collective-permute-start.7
  210.0 47.0 %copy-start.3 = (bf16[2,4,48,1280]{3,2,1,0:T(8,128)(2,1)}, bf16[2,4,48,1280]{3,2,1,0:T(8,128)(2,1)S(1)}, u32[]{:S(2)}) copy-start(bf16[2,4,48,1280]{3,2,1,0:T(8,128)(2,1)S(1)} %get-tuple-element.223) | copy-start | bytes 2949124
  994.4 5.5 copy-start
  1009.2 5.5 copy-start
  1024.0 5.5 copy-start
  1038.8 5.5 copy-start
  1053.7 5.5 copy-start
  1068.5 5.5 copy-start
  1083.3 5.5 copy-start
  1098.1 5.5 copy-start
  1112.9 5.5 copy-start
  1127.8 5.5 copy-start
  1142.6 5.5 copy-start
  1157.4 5.5 copy-start
  1172.2 5.5 copy-start
  1187.0 5.5 copy-start
  1201.9 5.5 copy-start
  1216.7 5.5 copy-start
  1231.5 5.5 copy-start
  1246.3 5.5 copy-start
  1275.9 5.5 copy-start
  1290.8 5.5 copy-start
  1320.4 5.5 copy-start
  1394.5 5.5 copy-start
  1409.3 5.5 copy-start
  1424.1 5.5 copy-start
  1439.0 5.5 copy-start
  1468.7 49.1 %copy-start.5 = (f32[1280]{0:T(1024)S(1)}, f32[1280]{0:T(1024)}, u32[]{:S(2)}) copy-start(f32[1280]{0:T(1024)} %get-tuple-element.199) | copy-start | bytes 15364
  1468.7 49.1 %copy-start.6 = (f32[1280]{0:T(1024)S(1)}, f32[1280]{0:T(1024)}, u32[]{:S(2)}) copy-start(f32[1280]{0:T(1024)} %get-tuple-element.200) | copy-start | bytes 15364
  1517.8 14.5 copy-start.11
  1518.6 6.5 collective-permute-start.8
  1522.0 7.5 collective-permute-start.9
  1529.6 5.1 collective-permute-start.10
  1531.0 5.3 collective-permute-start.11
  1623.4 10.2 collective-permute-start.13
  1626.2 6.1 collective-permute-start.12
  1633.6 3.2 collective-permute-start.14
  1635.5 4.8 collective-permute-start.15
  (14 other events, 55.9 us)
Sparse Core Ops, SparseCore 0:
  275.6 346.7 all-gather.1
where the time goes:
time: 1690 us; the launch traced here: 1680 us
  local copies, waits for them, and re-layouts  428 us (25%)
  matrix products  398 us (24%)
  waiting for transfers between devices  372 us (22%)
  blocking collectives  231 us (14%)
  other arithmetic  196 us (12%)
  starting transfers between devices  34.6 us (2%)
    all_gather x1, waiting for transfers between devices, attn_block(): kv_all = lax.all_gather(qkv_loc[1:], ('row', 'col'), axis=2, tiled=True)  344 us
    unnamed x32, local copies, waits for them, and re-layouts  279 us
    psum x5, blocking collectives, group_norm(): lax.psum(part_sums, ('row', 'col')) / (n_rows * n_cols * group_ch * n_dev)  231 us
    dot_general x32, matrix products, key_step(): jnp.einsum('bqhd,bkhd->bhqk', queries, key_blk, preferred_element_type=jn...  194 us
    reduce_sum x32, other arithmetic, key_step(): run_sum = run_sum * rescale + jnp.sum(exp_logits, axis=-1)  164 us
    dot_general x32, matrix products, key_step(): jnp.einsum('bhqk,bkhd->bhqd', exp_logits.astype(jnp.bfloat16), val_blk, p...  103 us
    slice x1, local copies, waits for them, and re-layouts, attn_block(): kv_all[1]  94.5 us
    conv_general_dilated x4, matrix products, halo_conv(): lax.conv_general_dilated(padded, kernel, (1, 1), 'VALID', dimension_numbe...  82.2 us
  transfers between devices with their start and end apart: 17, of which 13 were waited for; matrix products, arithmetic and copies ran while one was open for 1% of the time, Pallas kernels for 0%

commit v1 on v0

v1 whole, which is shorter than its diff:
```python
import functools

import jax
import jax.numpy as jnp
from jax import lax
from jax.experimental import pallas as pl
from jax.experimental.pallas import tpu as pltpu
from jax.sharding import PartitionSpec as P

GROUPS = 32
EPS = 1e-5
LANES = 128
MESH = pl.DeviceIdType.MESH
HIGH = lax.Precision.HIGHEST
F32 = jnp.float32
BF16 = jnp.bfloat16
VMEM_LIMIT = 60 * 1024 * 1024
VSPEC = pl.BlockSpec(memory_space=pltpu.VMEM)
ASPEC = pl.BlockSpec(memory_space=pl.ANY)


def group_mask(n_chan, chan_axis):
    width = n_chan // GROUPS
    shape = (n_chan, LANES) if chan_axis == 0 else (LANES, n_chan)
    chan = lax.broadcasted_iota(jnp.int32, shape, chan_axis)
    first = lax.broadcasted_iota(jnp.int32, shape, 1 - chan_axis) * width
    return jnp.where((chan >= first) & (chan < first + width), 1.0, 0.0).astype(F32)


def channel_stats(tot, count):
    vals = tot / count
    mean = vals[0:2]
    inv = lax.rsqrt(vals[2:4] - mean * mean + EPS)
    return jnp.concatenate([mean, inv, jnp.zeros((4, LANES), F32)], axis=0)


def expand(stats, n_chan):
    return jnp.dot(stats, group_mask(n_chan, 1), precision=HIGH, preferred_element_type=F32)


def silu(u):
    half = 0.5 * u
    return half * jnp.tanh(half) + half


def finish(acc, out_ref, edge_ref, part_ref, csum):
    n_img, n_rows, n_cols, n_chan = out_ref.shape
    per_img = n_rows * n_cols
    csum[...] = jnp.zeros_like(csum)
    for ch in range(0, n_chan, 256):
        sl = slice(ch, ch + 256)
        for b in range(n_img):
            val = acc[b * per_img:(b + 1) * per_img, sl].astype(BF16)
            out_ref[b, :, :, sl] = val.reshape(n_rows, n_cols, 256)
            val = val.astype(F32)
            csum[b:b + 1, sl] = jnp.sum(val, axis=0, keepdims=True)
            csum[2 + b:3 + b, sl] = jnp.sum(val * val, axis=0, keepdims=True)
    for side, col in ((0, 0), (1, n_cols - 1)):
        for i in range(n_rows):
            rows = [acc[b * per_img + i * n_cols + col:b * per_img + i * n_cols + col + 1, :] for b in range(n_img)]
            edge_ref[side, i] = jnp.concatenate(rows, axis=0).astype(BF16)
    part_ref[...] = jnp.dot(csum[...], group_mask(n_chan, 0), precision=HIGH, preferred_element_type=F32)


def prep_kernel(x_ref, edge_ref, part_ref, acc, dump, csum):
    n_img, n_rows, n_cols, n_chan = x_ref.shape
    acc[...] = x_ref[...].reshape(acc.shape).astype(F32)
    finish(acc, dump, edge_ref, part_ref, csum)


def finish_shapes(shape):
    n_img, n_rows, n_cols, n_chan = shape
    return [jax.ShapeDtypeStruct((2, n_rows, n_img, n_chan), BF16), jax.ShapeDtypeStruct((8, LANES), F32)]


def prep(x):
    n_tok = x.shape[0] * x.shape[1] * x.shape[2]
    return pl.pallas_call(
        prep_kernel,
        out_shape=finish_shapes(x.shape),
        in_specs=[VSPEC],
        out_specs=[VSPEC, VSPEC],
        scratch_shapes=[pltpu.VMEM((n_tok, x.shape[3]), F32), pltpu.VMEM(x.shape, BF16), pltpu.VMEM((8, x.shape[3]), F32)],
        compiler_params=pltpu.CompilerParams(vmem_limit_bytes=VMEM_LIMIT),
        name="prep",
    )(x)


def exchange_kernel(n_row, n_col, halo, *refs):
    if halo:
        part_ref, x_ref, edge_ref, tot_ref, top_ref, bot_ref, side_ref, rbuf, cbuf, rsum, send, recv = refs
    else:
        part_ref, tot_ref, rbuf, cbuf, rsum, send, recv = refs
    r, c = lax.axis_index('row'), lax.axis_index('col')
    up, down = lax.rem(r + n_row - 1, n_row), lax.rem(r + 1, n_row)
    left, right = lax.rem(c + n_col - 1, n_col), lax.rem(c + 1, n_col)
    row_peers = [{'row': lax.rem(r + k, n_row)} for k in range(1, n_row)]
    col_peers = [{'col': lax.rem(c + k, n_col)} for k in range(1, n_col)]
    diag = [{'row': a, 'col': b} for a in (up, down) for b in (left, right)] if halo else []
    peers = row_peers + col_peers + diag
    barrier = pltpu.get_barrier_semaphore()
    for peer in peers:
        pl.semaphore_signal(barrier, inc=1, device_id=peer, device_id_type=MESH)
    pl.semaphore_wait(barrier, len(peers))

    def copy(src, dst, slot, peer):
        return pltpu.make_async_remote_copy(src_ref=src, dst_ref=dst, send_sem=send.at[slot], recv_sem=recv.at[slot], device_id=peer, device_id_type=MESH)

    first = [copy(part_ref, rbuf.at[k], k, row_peers[k]) for k in range(n_row - 1)]
    for cp in first:
        cp.start()
    base = n_row - 1 + n_col - 1
    halos = []
    if halo:
        last = x_ref.shape[1] - 1
        end = side_ref.shape[1] - 1
        plan = [
            (x_ref.at[:, last], top_ref, {'row': down}),
            (x_ref.at[:, 0], bot_ref, {'row': up}),
            (edge_ref.at[0], side_ref.at[1, 1:end], {'col': left}),
            (edge_ref.at[1], side_ref.at[0, 1:end], {'col': right}),
            (edge_ref.at[0, 0], side_ref.at[1, end], {'row': up, 'col': left}),
            (edge_ref.at[0, last], side_ref.at[1, 0], {'row': down, 'col': left}),
            (edge_ref.at[1, 0], side_ref.at[0, end], {'row': up, 'col': right}),
            (edge_ref.at[1, last], side_ref.at[0, 0], {'row': down, 'col': right}),
        ]
        halos = [copy(src, dst, base + i, peer) for i, (src, dst, peer) in enumerate(plan)]
        for cp in halos:
            cp.start()
    total = part_ref[...]
    for k, cp in enumerate(first):
        cp.wait_recv()
        total = total + rbuf[k]
    rsum[...] = total
    second = [copy(rsum, cbuf.at[k], n_row - 1 + k, col_peers[k]) for k in range(n_col - 1)]
    for cp in second:
        cp.start()
    for k, cp in enumerate(second):
        cp.wait_recv()
        total = total + cbuf[k]
    tot_ref[...] = total
    for cp in halos:
        cp.wait_recv()
    for cp in first + second + halos:
        cp.wait_send()


def exchange(part, n_row, n_col, x=None, edge=None):
    halo = x is not None
    out_shape = [jax.ShapeDtypeStruct((8, LANES), F32)]
    args = [part]
    in_specs = [VSPEC]
    if halo:
        n_img, n_rows, n_cols, n_chan = x.shape
        out_shape += [
            jax.ShapeDtypeStruct((n_img, n_cols, n_chan), BF16),
            jax.ShapeDtypeStruct((n_img, n_cols, n_chan), BF16),
            jax.ShapeDtypeStruct((2, n_rows + 2, n_img, n_chan), BF16),
        ]
        args += [x, edge]
        in_specs += [ASPEC, VSPEC]
    n_sem = n_row + n_col - 2 + (8 if halo else 0)
    return pl.pallas_call(
        functools.partial(exchange_kernel, n_row, n_col, halo),
        out_shape=out_shape,
        in_specs=in_specs,
        out_specs=[VSPEC] * len(out_shape),
        scratch_shapes=[
            pltpu.VMEM((n_row - 1, 8, LANES), F32),
            pltpu.VMEM((n_col - 1, 8, LANES), F32),
            pltpu.VMEM((8, LANES), F32),
            pltpu.SemaphoreType.DMA((n_sem,)),
            pltpu.SemaphoreType.DMA((n_sem,)),
        ],
        compiler_params=pltpu.CompilerParams(collective_id=1 if halo else 2, has_side_effects=True, vmem_limit_bytes=16 * 1024 * 1024),
        name="exchange",
    )(*args)


def conv_kernel(blk, idx, n_row, n_col, count, residual, x_ref, top_ref, bot_ref, side_ref, tot_ref, norm_ref, add_ref, w_hbm,
                out_ref, edge_ref, part_ref, act, hside, stat, wbuf, acc, csum, sem):
    n_img, n_rows, n_cols, n_chan = x_ref.shape
    per_img = n_rows * n_cols

    def fetch(dy):
        return pltpu.make_async_copy(w_hbm.at[blk, idx, dy], wbuf.at[dy], sem.at[dy])

    for dy in range(3):
        fetch(dy).start()
    r, c = lax.axis_index('row'), lax.axis_index('col')
    st = expand(channel_stats(tot_ref[...], count), n_chan)
    gain = norm_ref[blk, idx, 0:1, :].astype(F32)
    shift = norm_ref[blk, idx, 1:2, :].astype(F32)
    stat[0:2] = st[0:2]
    stat[2:4] = st[2:4] * gain
    stat[4:5] = shift

    for side in range(2):
        inside = (c > 0) if side == 0 else (c < n_col - 1)
        for i in range(n_rows + 2):
            ok = inside
            if i == 0:
                ok = ok & (r > 0)
            if i == n_rows + 1:
                ok = ok & (r < n_row - 1)
            z = side_ref[side, i].astype(F32)
            a = silu((z - stat[0:2]) * stat[2:4] + stat[4:5])
            hside[side, i] = jnp.where(ok, a, 0.0)

    step = 256

    def place(b, i, src, ok):
        rows = lax.broadcasted_iota(jnp.int32, (n_cols, step), 0)
        for ch in range(0, n_chan, step):
            sl = slice(ch, ch + step)
            z = src(sl).astype(F32)
            a = silu((z - stat[b:b + 1, sl]) * stat[2 + b:3 + b, sl] + stat[4:5, sl])
            if ok is not None:
                a = jnp.where(ok, a, 0.0)
            act[b, i, :, n_chan + ch:n_chan + ch + step] = a.astype(BF16)
            lo = jnp.where(rows == 0, hside[0, i, b:b + 1, sl], pltpu.roll(a, 1, 0))
            act[b, i, :, ch:ch + step] = lo.astype(BF16)
            hi = jnp.where(rows == n_cols - 1, hside[1, i, b:b + 1, sl], pltpu.roll(a, n_cols - 1, 0))
            act[b, i, :, 2 * n_chan + ch:2 * n_chan + ch + step] = hi.astype(BF16)

    for b in range(n_img):
        place(b, 0, lambda sl, b=b: top_ref[b, :, sl], r > 0)

        def middle(i, carry, b=b):
            place(b, i + 1, lambda sl: x_ref[b, i, :, sl], None)
            return carry

        lax.fori_loop(0, n_rows, middle, 0)
        place(b, n_rows + 1, lambda sl, b=b: bot_ref[b, :, sl], r < n_row - 1)

    if residual:
        acc[...] = add_ref[...].reshape(acc.shape).astype(F32)
    else:
        for b in range(n_img):
            acc[b * per_img:(b + 1) * per_img, :] = jnp.broadcast_to(add_ref[b:b + 1, :], (per_img, n_chan))

    def taps(dy, carry):
        fetch(dy).wait()
        lhs = act[:, pl.ds(dy, n_rows)].reshape(n_img * per_img, 3 * n_chan)
        for ch in range(0, n_chan, 256):
            rhs = wbuf[dy, :, :, ch:ch + 256].reshape(3 * n_chan, 256)
            acc[:, ch:ch + 256] += jnp.dot(lhs, rhs, preferred_element_type=F32)
        return carry

    lax.fori_loop(0, 3, taps, 0)
    finish(acc, out_ref, edge_ref, part_ref, csum)


def conv(blk, idx, x, halos, norm, add, weights, n_row, n_col, residual):
    tot, top, bot, side = halos
    n_img, n_rows, n_cols, n_chan = x.shape
    count = float(n_rows * n_cols * n_row * n_col * (n_chan // GROUPS))
    n_tok = n_img * n_rows * n_cols
    return pl.pallas_call(
        functools.partial(conv_kernel, blk, idx, n_row, n_col, count, residual),
        out_shape=[jax.ShapeDtypeStruct(x.shape, BF16)] + finish_shapes(x.shape),
        in_specs=[VSPEC] * 7 + [ASPEC],
        out_specs=[VSPEC] * 3,
        scratch_shapes=[
            pltpu.VMEM((n_img, n_rows + 2, n_cols, 3 * n_chan), BF16),
            pltpu.VMEM((2, n_rows + 2, n_img, n_chan), F32),
            pltpu.VMEM((8, n_chan), F32),
            pltpu.VMEM((3, 3, n_chan, n_chan), BF16),
            pltpu.VMEM((n_tok, n_chan), F32),
            pltpu.VMEM((8, n_chan), F32),
            pltpu.SemaphoreType.DMA((3,)),
        ],
        compiler_params=pltpu.CompilerParams(vmem_limit_bytes=VMEM_LIMIT),
        cost_estimate=pl.CostEstimate(flops=2 * 9 * n_tok * n_chan * n_chan, bytes_accessed=9 * 2 * n_chan * n_chan, transcendentals=n_tok * n_chan),
        name="conv",
    )(x, top, bot, side, tot, norm, add, weights)


def proj_kernel(count, per_dev, x_ref, tot_ref, norm_ref, w_ref, out_ref, g, wcat):
    n_img, n_rows, n_cols, n_chan = x_ref.shape
    per_img = n_rows * n_cols
    hd = w_ref.shape[2]

    @pl.when(pl.program_id(0) == 0)
    def _():
        st = expand(channel_stats(tot_ref[...], count), n_chan)
        gain = norm_ref[0:1, :].astype(F32)
        shift = norm_ref[1:2, :].astype(F32)
        for b in range(n_img):
            z = x_ref[b].reshape(per_img, n_chan).astype(F32)
            g[b * per_img:(b + 1) * per_img, :] = ((z - st[b:b + 1]) * (st[2 + b:3 + b] * gain) + shift).astype(BF16)
        wcat[per_dev * 3 * hd:, :] = jnp.zeros((wcat.shape[0] - per_dev * 3 * hd, n_chan), BF16)

    for i in range(per_dev):
        wcat[2 * i * hd:(2 * i + 1) * hd, :] = w_ref[1, i]
        wcat[(2 * i + 1) * hd:(2 * i + 2) * hd, :] = w_ref[2, i]
        wcat[(2 * per_dev + i) * hd:(2 * per_dev + i + 1) * hd, :] = w_ref[0, i]
    for n in range(0, wcat.shape[0], 256):
        res = lax.dot_general(g[...], wcat[n:n + 256, :], (((1,), (1,)), ((), ())), preferred_element_type=F32).astype(BF16)
        for b in range(n_img):
            out_ref[b, 0, :, n:n + 256] = res[b * per_img:(b + 1) * per_img]


def proj(x, tot, norm, weights, n_row, n_col, per_dev):
    n_img, n_rows, n_cols, n_chan = x.shape
    _, n_heads, hd, _ = weights.shape
    count = float(n_rows * n_cols * n_row * n_col * (n_chan // GROUPS))
    n_grp = n_heads // per_dev
    width = -(-per_dev * 3 * hd // 256) * 256
    return pl.pallas_call(
        functools.partial(proj_kernel, count, per_dev),
        grid=(n_grp,),
        out_shape=jax.ShapeDtypeStruct((n_img, n_grp, n_rows * n_cols, width), BF16),
        in_specs=[
            pl.BlockSpec(x.shape, lambda q: (0, 0, 0, 0)),
            pl.BlockSpec((8, LANES), lambda q: (0, 0)),
            pl.BlockSpec(norm.shape, lambda q: (0, 0)),
            pl.BlockSpec((3, per_dev, hd, n_chan), lambda q: (0, q, 0, 0)),
        ],
        out_specs=pl.BlockSpec((n_img, 1, n_rows * n_cols, width), lambda q: (0, q, 0, 0)),
        scratch_shapes=[pltpu.VMEM((n_img * n_rows * n_cols, n_chan), BF16), pltpu.VMEM((width, n_chan), BF16)],
        compiler_params=pltpu.CompilerParams(vmem_limit_bytes=VMEM_LIMIT),
        name="proj",
    )(x, tot, norm, weights)


def attend_kernel(hd, q_ref, kv_ref, out_ref, qt, vt, ot, qf):
    n_q, n_k = q_ref.shape[0], kv_ref.shape[0]
    half = lax.rem(pl.program_id(0), 2)
    factor = 1.4426950408889634 * hd ** -0.5
    kb, qb = min(1024, n_k), min(512, n_q)
    tb = min(512, n_q)
    for t in range(0, n_q, tb):
        qf[:, t:t + tb] = q_ref[t:t + tb, :].astype(F32).T
    qt[0:hd, :] = qf[pl.ds(pl.multiple_of(half * hd, hd), hd), :].astype(BF16)
    qt[hd:, :] = jnp.zeros((qt.shape[0] - hd, n_q), BF16)

    def flip(t, carry):
        at = pl.multiple_of(t * tb, tb)
        vt[:, pl.ds(at, tb)] = kv_ref[pl.ds(at, tb), :].astype(F32).T[hd:].astype(BF16)
        return carry

    lax.fori_loop(0, n_k // tb, flip, 0)

    def queries(t, carry):
        at = pl.multiple_of(t * qb, qb)
        rhs = qt[:, pl.ds(at, qb)]

        def keys(s, state):
            run_max, run_sum, out = state
            pos = pl.multiple_of(s * kb, kb)
            logits = jnp.dot(kv_ref[pl.ds(pos, kb), :], rhs, preferred_element_type=F32)
            new_max = jnp.maximum(run_max, jnp.max(logits, axis=0, keepdims=True))
            scale = jnp.exp2((run_max - new_max) * factor)
            w = jnp.exp2((logits - new_max) * factor)
            run_sum = run_sum * scale + jnp.sum(w, axis=0, keepdims=True)
            out = out * scale + jnp.dot(vt[:, pl.ds(pos, kb)], w.astype(BF16), preferred_element_type=F32)
            return new_max, run_sum, out

        init = (jnp.full((1, qb), -jnp.inf, F32), jnp.zeros((1, qb), F32), jnp.zeros((hd, qb), F32))
        _, run_sum, out = lax.fori_loop(0, n_k // kb, keys, init)
        ot[pl.ds(pl.multiple_of(half * hd, hd), hd), pl.ds(at, qb)] = out / run_sum
        return carry

    lax.fori_loop(0, n_q // qb, queries, 0)
    for t in range(0, n_q, tb):
        out_ref[t:t + tb, :] = ot[:, t:t + tb].T.astype(BF16)


def attend(q, kv, hd, per_dev):
    n_q, n_k = q.shape[0], kv.shape[0]
    return pl.pallas_call(
        functools.partial(attend_kernel, hd),
        grid=(per_dev,),
        out_shape=jax.ShapeDtypeStruct(q.shape, BF16),
        in_specs=[pl.BlockSpec((n_q, 2 * hd), lambda i: (0, i // 2)), pl.BlockSpec((n_k, 2 * hd), lambda i: (0, i))],
        out_specs=pl.BlockSpec((n_q, 2 * hd), lambda i: (0, i // 2)),
        scratch_shapes=[pltpu.VMEM((2 * hd, n_q), BF16), pltpu.VMEM((hd, n_k), BF16), pltpu.VMEM((2 * hd, n_q), F32), pltpu.VMEM((2 * hd, n_q), F32)],
        compiler_params=pltpu.CompilerParams(vmem_limit_bytes=VMEM_LIMIT),
        name="attend",
    )(q, kv)


def outproj_kernel(o_ref, w_ref, x_ref, out_ref, edge_ref, part_ref, wcat, acc, csum):
    n_img, n_rows, n_cols, n_chan = x_ref.shape
    per_dev, hd, _ = w_ref.shape[1:]
    per_img = n_rows * n_cols
    q = pl.program_id(0)

    @pl.when(q == 0)
    def _():
        acc[...] = x_ref[...].reshape(acc.shape).astype(F32)
        wcat[per_dev * hd:, :] = jnp.zeros((wcat.shape[0] - per_dev * hd, n_chan), BF16)

    for i in range(per_dev):
        wcat[i * hd:(i + 1) * hd, :] = w_ref[0, i]
    lhs = o_ref[:, 0].reshape(n_img * per_img, o_ref.shape[3])
    for n in range(0, n_chan, 256):
        acc[:, n:n + 256] += jnp.dot(lhs, wcat[:, n:n + 256], preferred_element_type=F32)

    @pl.when(q == pl.num_programs(0) - 1)
    def _():
        finish(acc, out_ref, edge_ref, part_ref, csum)


def outproj(o, weights, x, per_dev):
    n_img, n_grp, n_tok, width = o.shape
    _, n_heads, hd, n_chan = weights.shape
    shapes = [jax.ShapeDtypeStruct(x.shape, BF16)] + finish_shapes(x.shape)
    return pl.pallas_call(
        outproj_kernel,
        grid=(n_grp,),
        out_shape=shapes,
        in_specs=[
            pl.BlockSpec((n_img, 1, n_tok, width), lambda q: (0, q, 0, 0)),
            pl.BlockSpec((1, per_dev, hd, n_chan), lambda q: (3, q, 0, 0)),
            pl.BlockSpec(x.shape, lambda q: (0, 0, 0, 0)),
        ],
        out_specs=[pl.BlockSpec(s.shape, lambda q, n=len(s.shape): (0,) * n) for s in shapes],
        scratch_shapes=[pltpu.VMEM((width, n_chan), BF16), pltpu.VMEM((n_img * n_tok, n_chan), F32), pltpu.VMEM((8, n_chan), F32)],
        compiler_params=pltpu.CompilerParams(vmem_limit_bytes=VMEM_LIMIT),
        name="outproj",
    )(o, weights, x)


def solution(mesh):
    n_row, n_col = mesh.shape['row'], mesh.shape['col']

    def res_block(blk, x, edge, part, t_emb, res_norm, res_conv, res_temb):
        t_act = jax.nn.silu(t_emb.astype(F32)).astype(BF16)
        t_proj = jnp.dot(t_act, res_temb[blk], preferred_element_type=F32)
        halos = exchange(part, n_row, n_col, x, edge)
        h, edge, part = conv(blk, 0, x, halos, res_norm, t_proj, res_conv, n_row, n_col, False)
        halos = exchange(part, n_row, n_col, h, edge)
        return conv(blk, 1, h, halos, res_norm, x, res_conv, n_row, n_col, True)

    def attn_block(x, part, norm, weights):
        n_img, n_rows, n_cols, n_chan = x.shape
        weights = jnp.swapaxes(weights, 2, 3)
        n_heads, hd = weights.shape[1], weights.shape[2]
        per_dev = n_img * n_heads // n_row
        n_tok = n_rows * n_cols
        tot, = exchange(part, n_row, n_col)
        qkv = proj(x, tot, norm, weights, n_row, n_col, per_dev)
        qkv = lax.all_to_all(qkv.reshape(n_row, n_tok, -1), 'row', 0, 0).reshape(n_row * n_tok, -1)
        kv_width = per_dev * 2 * hd
        q_width = -(-per_dev // 2) * 2 * hd
        kv = lax.all_gather(qkv[:, :kv_width], 'col', axis=0, tiled=True)
        out = attend(qkv[:, kv_width:kv_width + q_width], kv, hd, per_dev)
        out = lax.all_to_all(out.reshape(n_row, n_tok, q_width), 'row', 0, 0)
        return outproj(out.reshape(n_img, -1, n_tok, q_width), weights, x, per_dev)

    def run_stage(latent, t_emb, res_norm, res_conv, res_temb, attn_norm, attn_proj):
        edge, part = prep(latent)
        x, edge, part = res_block(0, latent, edge, part, t_emb, res_norm, res_conv, res_temb)
        x, edge, part = attn_block(x, part, attn_norm, attn_proj)
        return res_block(1, x, edge, part, t_emb, res_norm, res_conv, res_temb)[0]

    spec_x = P('dp', 'row', 'col', None)
    return jax.shard_map(run_stage, mesh=mesh, in_specs=(spec_x, P('dp', None), P(), P(), P(), P(), P()), out_specs=spec_x, check_vma=False)
```

time: 1690 us -> 430 us (0.25)
  local copies, waits for them, and re-layouts: 428 us -> 26.2 us
  matrix products: 398 us -> 6.17 us
  waiting for transfers between devices: 372 us -> 87.2 us
  Pallas kernels: 0 us -> 248 us
  other arithmetic: 196 us -> 0 us
  blocking collectives: 231 us -> 42.1 us
  starting transfers between devices: 34.6 us -> 5.19 us
    dot_general x68 -> x2, matrix products: 315 us -> 6.17 us  [res_block(): t_proj = jnp.dot(t_act, res_temb[blk], preferred_element_type=F32)]
    all_gather x1, waiting for transfers between devices: 344 us -> 74 us  [attn_block(): kv = lax.all_gather(qkv[:, :kv_width], 'col', axis=0, tiled=True)]
    unnamed x32 -> x64, local copies, waits for them, and re-layouts: 279 us -> 23.4 us
    pallas_call x0 -> x13, Pallas kernels: none -> 248 us  [the longest x1 102 us: attend(): pl.pallas_call(functools.partial(attend_kernel, hd), grid=(per_dev,), out...]
    psum x5 -> x0, blocking collectives: 231 us -> none  [group_norm(): lax.psum(part_sums, ('row', 'col')) / (n_rows * n_cols * group_ch * n_dev)]
    reduce_sum x48 -> x0, other arithmetic: 168 us -> none  [the longest x32 164 us: key_step(): run_sum = run_sum * rescale + jnp.sum(exp_logits, axis=-1)]
    slice x11 -> x2, local copies, waits for them, and re-layouts: 103 us -> 2.75 us  [the longest x1 1.56 us: attn_block(): kv = lax.all_gather(qkv[:, :kv_width], 'col', axis=0, tiled=True)]
    conv_general_dilated x4 -> x0, matrix products: 82.2 us -> none  [halo_conv(): lax.conv_general_dilated(padded, kernel, (1, 1), 'VALID', dimension_numbe...]
  transfers between devices with their start and end apart: 17 -> 2, of which waited for: 13 -> 2; matrix products, arithmetic and copies ran while one was open for 1% -> 1% of each run, Pallas kernels for 0% -> 0%
where the time goes in v1:
time: 430 us; the launch traced here: 429 us
  Pallas kernels  248 us (58%)
  waiting for transfers between devices  87.2 us (20%)
  blocking collectives  42.1 us (10%)
  local copies, waits for them, and re-layouts  26.2 us (6%)
  between operations  13.6 us (3%)
  matrix products  6.17 us (1%)
  starting transfers between devices  5.19 us (1%)
    pallas_call x1, Pallas kernels, attend(): pl.pallas_call(functools.partial(attend_kernel, hd), grid=(per_dev,), out...  102 us
    pallas_call x4, Pallas kernels, conv(): pl.pallas_call(functools.partial(conv_kernel, blk, idx, n_row, n_col, cou...  76.1 us
    all_gather x1, waiting for transfers between devices, attn_block(): kv = lax.all_gather(qkv[:, :kv_width], 'col', axis=0, tiled=True)  74 us
    pallas_call x5, Pallas kernels, exchange(): pl.pallas_call(functools.partial(exchange_kernel, n_row, n_col, halo), ou...  51.2 us
    all_to_all x1, blocking collectives, attn_block(): lax.all_to_all(qkv.reshape(n_row, n_tok, -1), 'row', 0, 0)  42.1 us
    unnamed x64, local copies, waits for them, and re-layouts  23.4 us
    all_to_all x1, waiting for transfers between devices, attn_block(): out = lax.all_to_all(out.reshape(n_row, n_tok, q_width), 'row', 0, 0)  13.1 us
    pallas_call x1, Pallas kernels, proj(): pl.pallas_call(functools.partial(proj_kernel, count, per_dev), grid=(n_gr...  9.47 us
  transfers between devices with their start and end apart: 2, of which 2 were waited for; matrix products, arithmetic and copies ran while one was open for 1% of the time, Pallas kernels for 0%

profile of v1, /device:TPU:97, one launch (start us, length us, event | category | flops | bytes accessed | tf_op | source)
XLA Modules:
  0.0 428.6 jit_solution(5265433478814119869)
XLA Ops:
  6.6 2.7 prep.1
  9.2 1.2 copy-done
  10.4 0.8 copy-done.19
  11.2 0.7 copy-done.28
  11.9 13.8 %exchange.5 = (f32[8,128]{1,0:T(8,128)S(1)}, bf16[2,48,1280]{2,1,0:T(8,128)(2,1)S(1)}, bf16[2,48,1280]{2,1,0:T(8,128)(2,1)S(1)}, bf16[2,6,2,1280]{3,2,1,0:T(2,128)(2,1)S(1)}) custom-call(f32[8,128]{1,0:T(8,128)S(1)} %copy-done.28, bf16[2,4,48,1280]{3,2,1,0:T(8,128)(2,1)S(1)} %copy-done, bf16[2,4,2,1280]{3,2,1,0:T(2,128)(2,1)S(1)} %copy-done.19), custom_call_target="tpu_custom_call" | custom-call | tf_op jit(solution)/shard_map/exchange/pallas_call | solution.py:163
  25.7 0.7 copy-done.6
  26.4 0.7 copy-done.7
  27.1 0.6 copy-done.13
  27.8 0.6 copy-done.22
  28.3 3.1 fusion.2.add_ref
  31.4 18.8 %conv.4 = (bf16[2,4,48,1280]{3,2,1,0:T(8,128)(2,1)}, bf16[2,4,2,1280]{3,2,1,0:T(2,128)(2,1)}, f32[8,128]{1,0:T(8,128)}) custom-call(bf16[2,4,48,1280]{3,2,1,0:T(8,128)(2,1)} %add_ref.1, bf16[2,48,1280]{2,1,0:T(8,128)(2,1)} %copy-done.6, bf16[2,48,1280]{2,1,0:T(8,128)(2,1)} %copy-done.7, bf16[2,6,2,1280]{3,2,1,0:T(2,128)(2,1)} %copy-done.13, ...), custom_call_target="tpu_custom_call" | custom-call | flops 11324620800 | bytes 29491200 | tf_op jit(solution)/shard_map/conv/pallas_call | solution.py:259
  50.3 1.2 copy-done.3
  51.5 0.8 copy-done.16
  52.3 0.7 copy-done.25
  52.9 9.6 %exchange.6 = (f32[8,128]{1,0:T(8,128)S(1)}, bf16[2,48,1280]{2,1,0:T(8,128)(2,1)S(1)}, bf16[2,48,1280]{2,1,0:T(8,128)(2,1)S(1)}, bf16[2,6,2,1280]{3,2,1,0:T(2,128)(2,1)S(1)}) custom-call(f32[8,128]{1,0:T(8,128)S(1)} %copy-done.25, bf16[2,4,48,1280]{3,2,1,0:T(8,128)(2,1)S(1)} %copy-done.3, bf16[2,4,2,1280]{3,2,1,0:T(2,128)(2,1)S(1)} %copy-done.16), custom_call_target="tpu_custom_call" | custom-call | tf_op jit(solution)/shard_map/exchange/pallas_call | solution.py:163
  62.5 0.7 copy-done.8
  63.2 0.7 copy-done.9
  63.9 0.6 copy-done.14
  65.2 19.2 %conv.5 = (bf16[2,4,48,1280]{3,2,1,0:T(8,128)(2,1)}, bf16[2,4,2,1280]{3,2,1,0:T(2,128)(2,1)}, f32[8,128]{1,0:T(8,128)}) custom-call(bf16[2,4,48,1280]{3,2,1,0:T(8,128)(2,1)} %get-tuple-element.41.refs_1_.x_ref, bf16[2,48,1280]{2,1,0:T(8,128)(2,1)} %copy-done.8, bf16[2,48,1280]{2,1,0:T(8,128)(2,1)} %copy-done.9, bf16[2,6,2,1280]{3,2,1,0:T(2,128)(2,1)} %copy-done.14, ...), custom_call_target="tpu_custom_call" | custom-call | flops 11324620800 | bytes 29491200 | tf_op jit(solution)/shard_map/conv/pallas_call | solution.py:259
  84.4 0.7 copy-done.29
  85.1 8.8 %exchange.7.tot_ref = f32[8,128]{1,0:T(8,128)S(1)} custom-call(f32[8,128]{1,0:T(8,128)S(1)} %copy-done.29), custom_call_target="tpu_custom_call" | custom-call | tf_op jit(solution)/shard_map/exchange/pallas_call | solution.py:163
  94.5 9.5 %proj.1 = bf16[2,4,192,1024]{3,2,1,0:T(8,128)(2,1)} custom-call(bf16[2,4,48,1280]{3,2,1,0:T(8,128)(2,1)} %get-tuple-element.48.x_ref, f32[8,128]{1,0:T(8,128)} %copy-done.20, bf16[2,1280]{1,0:T(2,128)(2,1)} %norm_ref.7, bf16[4,20,64,1280]{3,2,1,0:T(8,128)(2,1)} %bitcast.11), custom_call_target="tpu_custom_call" | custom-call | tf_op jit(solution)/shard_map/proj/pallas_call | solution.py:310
  103.9 42.1 %all_to_all.10 = bf16[8,192,1024]{2,1,0:T(8,128)(2,1)S(1)} all-to-all(bf16[8,192,1024]{2,1,0:T(8,128)(2,1)} %bitcast.15), channel_id=1, replica_groups=mesh['dp'=1,'col'=4,'row'=8] {'row'}, dimensions={0} | all-to-all | bytes 6291456 | tf_op jit(solution)/shard_map/all_to_all | solution.py:445
  146.0 1.6 slice.17
  147.7 1.2 slice.16.q_ref
  148.9 74.0 %all-gather.2.cloned.1.call-done.kv_ref = bf16[6144,640]{1,0:T(8,128)(2,1)} async-done(((bf16[1536,640]{1,0:T(8,128)(2,1)}), bf16[6144,640]{1,0:T(8,128)(2,1)}) %all-gather.2.cloned.1.call-update) | async-done | bytes 7864336 | tf_op jit(solution)/shard_map/all_gather | solution.py:448
  222.9 101.7 %attend.1 = bf16[1536,384]{1,0:T(8,128)(2,1)} custom-call(bf16[1536,384]{1,0:T(8,128)(2,1)} %slice.16.q_ref, bf16[6144,640]{1,0:T(8,128)(2,1)} %all-gather.2.cloned.1.call-done.kv_ref), custom_call_target="tpu_custom_call" | custom-call | tf_op jit(solution)/shard_map/attend/pallas_call | solution.py:372
  324.5 5.2 %all-to-all-start.1 = ((bf16[8,192,384]{2,1,0:T(8,128)(2,1)}), bf16[8,192,384]{2,1,0:T(8,128)(2,1)S(1)}, u32[]{:S(2)}, u32[]{:S(2)}) async-start(bf16[8,192,384]{2,1,0:T(8,128)(2,1)} %bitcast.16), calls=%async_computation.1 | async-start | bytes 2359296 | tf_op jit(solution)/shard_map/all_to_all | solution.py:450
  329.7 3.1 fusion.add_ref
  332.8 13.1 %all-to-all-done.1 = bf16[8,192,384]{2,1,0:T(8,128)(2,1)S(1)} async-done(((bf16[8,192,384]{2,1,0:T(8,128)(2,1)}), bf16[8,192,384]{2,1,0:T(8,128)(2,1)S(1)}, u32[]{:S(2)}, u32[]{:S(2)}) %all-to-all-start.1) | async-done | bytes 1179680 | tf_op jit(solution)/shard_map/all_to_all | solution.py:450
  345.9 1.0 copy-done.30
  346.9 7.0 %outproj.1 = (bf16[2,4,48,1280]{3,2,1,0:T(8,128)(2,1)}, bf16[2,4,2,1280]{3,2,1,0:T(2,128)(2,1)}, f32[8,128]{1,0:T(8,128)}) custom-call(bf16[2,4,192,384]{3,2,1,0:T(8,128)(2,1)} %bitcast.17, bf16[4,20,64,1280]{3,2,1,0:T(8,128)(2,1)} %bitcast.12, bf16[2,4,48,1280]{3,2,1,0:T(8,128)(2,1)} %get-tuple-element.48.x_ref), custom_call_target="tpu_custom_call" | custom-call | tf_op jit(solution)/shard_map/outproj/pallas_call | solution.py:410
  354.0 1.2 copy-done.1
  355.2 0.8 copy-done.18
  356.0 0.7 copy-done.27
  356.6 10.2 %exchange.8 = (f32[8,128]{1,0:T(8,128)S(1)}, bf16[2,48,1280]{2,1,0:T(8,128)(2,1)S(1)}, bf16[2,48,1280]{2,1,0:T(8,128)(2,1)S(1)}, bf16[2,6,2,1280]{3,2,1,0:T(2,128)(2,1)S(1)}) custom-call(f32[8,128]{1,0:T(8,128)S(1)} %copy-done.27, bf16[2,4,48,1280]{3,2,1,0:T(8,128)(2,1)S(1)} %copy-done.1, bf16[2,4,2,1280]{3,2,1,0:T(2,128)(2,1)S(1)} %copy-done.18), custom_call_target="tpu_custom_call" | custom-call | tf_op jit(solution)/shard_map/exchange/pallas_call | solution.py:163
  366.9 0.7 copy-done.10
  367.6 0.7 copy-done.11
  368.3 0.6 copy-done.15
  369.5 18.9 %conv.6 = (bf16[2,4,48,1280]{3,2,1,0:T(8,128)(2,1)}, bf16[2,4,2,1280]{3,2,1,0:T(2,128)(2,1)}, f32[8,128]{1,0:T(8,128)}) custom-call(bf16[2,4,48,1280]{3,2,1,0:T(8,128)(2,1)} %get-tuple-element.50.refs_1_.x_ref.add_ref, bf16[2,48,1280]{2,1,0:T(8,128)(2,1)} %copy-done.10, bf16[2,48,1280]{2,1,0:T(8,128)(2,1)} %copy-done.11, bf16[2,6,2,1280]{3,2,1,0:T(2,128)(2,1)} %copy-done.15, ...), custom_call_target="tpu_custom_call" | custom-call | flops 11324620800 | bytes 29491200 | tf_op jit(solution)/shard_map/conv/pallas_call | solution.py:259
  388.4 1.2 copy-done.2
  389.6 0.8 copy-done.17
  390.4 0.7 copy-done.26
  391.0 8.8 %exchange.9 = (f32[8,128]{1,0:T(8,128)S(1)}, bf16[2,48,1280]{2,1,0:T(8,128)(2,1)S(1)}, bf16[2,48,1280]{2,1,0:T(8,128)(2,1)S(1)}, bf16[2,6,2,1280]{3,2,1,0:T(2,128)(2,1)S(1)}) custom-call(f32[8,128]{1,0:T(8,128)S(1)} %copy-done.26, bf16[2,4,48,1280]{3,2,1,0:T(8,128)(2,1)S(1)} %copy-done.2, bf16[2,4,2,1280]{3,2,1,0:T(2,128)(2,1)S(1)} %copy-done.17), custom_call_target="tpu_custom_call" | custom-call | tf_op jit(solution)/shard_map/exchange/pallas_call | solution.py:163
  399.9 0.7 copy-done.4
  400.6 0.7 copy-done.5
  401.3 0.6 copy-done.12
  402.5 19.2 %conv.7 = (bf16[2,4,48,1280]{3,2,1,0:T(8,128)(2,1)}, bf16[2,4,2,1280]{3,2,1,0:T(2,128)(2,1)}, f32[8,128]{1,0:T(8,128)}) custom-call(bf16[2,4,48,1280]{3,2,1,0:T(8,128)(2,1)} %get-tuple-element.57.refs_1_.x_ref, bf16[2,48,1280]{2,1,0:T(8,128)(2,1)} %copy-done.4, bf16[2,48,1280]{2,1,0:T(8,128)(2,1)} %copy-done.5, bf16[2,6,2,1280]{3,2,1,0:T(2,128)(2,1)} %copy-done.12, ...), custom_call_target="tpu_custom_call" | custom-call | flops 11324620800 | bytes 29491200 | tf_op jit(solution)/shard_map/conv/pallas_call | solution.py:259
  (39 shorter events, 2.5 us)
Async XLA Ops:
  6.5 216.3 %all-gather.2.cloned.1.call-start = ((), (), s32[]{:S(2)}) async-start(), calls=%async_computation.2 | async-start | bytes 9830400 | tf_op jit(solution)/shard_map/all_gather | solution.py:448
  9.2 1.2 copy-start
  10.4 0.8 copy-start.19
  11.2 0.7 copy-start.28
  25.7 0.7 copy-start.6
  26.4 0.7 copy-start.7
  27.1 0.6 copy-start.13
  27.8 0.6 copy-start.22
  50.3 1.2 copy-start.3
  51.5 0.8 copy-start.16
  52.3 0.7 copy-start.25
  62.5 0.7 copy-start.8
  63.2 0.7 copy-start.9
  63.9 0.6 copy-start.14
  64.6 0.6 copy-start.23
  84.4 0.7 copy-start.29
  93.9 0.6 copy-start.20
  148.9 180.9 %copy-start.31 = (bf16[2,1280]{1,0:T(2,128)(2,1)S(1)}, bf16[2,1280]{1,0:T(2,128)(2,1)}, u32[]{:S(2)}) copy-start(bf16[2,1280]{1,0:T(2,128)(2,1)} %param.8) | copy-start | bytes 15364
  324.5 21.4 %all-to-all-start.1 = ((bf16[8,192,384]{2,1,0:T(8,128)(2,1)}), bf16[8,192,384]{2,1,0:T(8,128)(2,1)S(1)}, u32[]{:S(2)}, u32[]{:S(2)}) async-start(bf16[8,192,384]{2,1,0:T(8,128)(2,1)} %bitcast.16), calls=%async_computation.1 | async-start | bytes 2359296 | tf_op jit(solution)/shard_map/all_to_all | solution.py:450
  345.9 1.0 copy-start.30
  354.0 1.2 copy-start.1
  355.2 0.8 copy-start.18
  356.0 0.7 copy-start.27
  366.9 0.7 copy-start.10
  367.6 0.7 copy-start.11
  368.3 0.6 copy-start.15
  368.9 0.6 copy-start.24
  388.4 1.2 copy-start.2
  389.6 0.8 copy-start.17
  390.4 0.7 copy-start.26
  399.9 0.7 copy-start.4
  400.6 0.7 copy-start.5
  401.3 0.6 copy-start.12
  401.9 0.6 copy-start.21
Sparse Core Ops, SparseCore 0:
  147.8 75.0 all-gather.1

commit v2 on v1

--- a/solution.py
+++ b/solution.py
@@ -10,6 +10,8 @@
 GROUPS = 32
 EPS = 1e-5
 LANES = 128
+ROOM = 60.0
+TINY = 2.0 ** -90
 MESH = pl.DeviceIdType.MESH
 HIGH = lax.Precision.HIGHEST
 F32 = jnp.float32
@@ -88,16 +90,13 @@
 
 def exchange_kernel(n_row, n_col, halo, *refs):
     if halo:
-        part_ref, x_ref, edge_ref, tot_ref, top_ref, bot_ref, side_ref, rbuf, cbuf, rsum, send, recv = refs
+        part_ref, x_ref, edge_ref, tot_ref, top_ref, bot_ref, side_ref, buf, send, recv = refs
     else:
-        part_ref, tot_ref, rbuf, cbuf, rsum, send, recv = refs
+        part_ref, tot_ref, buf, send, recv = refs
     r, c = lax.axis_index('row'), lax.axis_index('col')
     up, down = lax.rem(r + n_row - 1, n_row), lax.rem(r + 1, n_row)
     left, right = lax.rem(c + n_col - 1, n_col), lax.rem(c + 1, n_col)
-    row_peers = [{'row': lax.rem(r + k, n_row)} for k in range(1, n_row)]
-    col_peers = [{'col': lax.rem(c + k, n_col)} for k in range(1, n_col)]
-    diag = [{'row': a, 'col': b} for a in (up, down) for b in (left, right)] if halo else []
-    peers = row_peers + col_peers + diag
+    peers = [{'row': lax.rem(r + i, n_row), 'col': lax.rem(c + j, n_col)} for i in range(n_row) for j in range(n_col) if i or j]
     barrier = pltpu.get_barrier_semaphore()
     for peer in peers:
         pl.semaphore_signal(barrier, inc=1, device_id=peer, device_id_type=MESH)
@@ -106,10 +105,9 @@
     def copy(src, dst, slot, peer):
         return pltpu.make_async_remote_copy(src_ref=src, dst_ref=dst, send_sem=send.at[slot], recv_sem=recv.at[slot], device_id=peer, device_id_type=MESH)
 
-    first = [copy(part_ref, rbuf.at[k], k, row_peers[k]) for k in range(n_row - 1)]
-    for cp in first:
+    copies = [copy(part_ref, buf.at[k], k, peer) for k, peer in enumerate(peers)]
+    for cp in copies:
         cp.start()
-    base = n_row - 1 + n_col - 1
     halos = []
     if halo:
         last = x_ref.shape[1] - 1
@@ -124,24 +122,17 @@
             (edge_ref.at[1, 0], side_ref.at[0, end], {'row': up, 'col': right}),
             (edge_ref.at[1, last], side_ref.at[0, 0], {'row': down, 'col': right}),
         ]
-        halos = [copy(src, dst, base + i, peer) for i, (src, dst, peer) in enumerate(plan)]
+        halos = [copy(src, dst, len(peers) + i, peer) for i, (src, dst, peer) in enumerate(plan)]
         for cp in halos:
             cp.start()
     total = part_ref[...]
-    for k, cp in enumerate(first):
+    for k, cp in enumerate(copies):
         cp.wait_recv()
-        total = total + rbuf[k]
-    rsum[...] = total
-    second = [copy(rsum, cbuf.at[k], n_row - 1 + k, col_peers[k]) for k in range(n_col - 1)]
-    for cp in second:
-        cp.start()
-    for k, cp in enumerate(second):
-        cp.wait_recv()
-        total = total + cbuf[k]
+        total = total + buf[k]
     tot_ref[...] = total
     for cp in halos:
         cp.wait_recv()
-    for cp in first + second + halos:
+    for cp in copies + halos:
         cp.wait_send()
 
 
@@ -159,20 +150,19 @@
         ]
         args += [x, edge]
         in_specs += [ASPEC, VSPEC]
-    n_sem = n_row + n_col - 2 + (8 if halo else 0)
+    n_peer = n_row * n_col - 1
+    n_sem = n_peer + (8 if halo else 0)
     return pl.pallas_call(
         functools.partial(exchange_kernel, n_row, n_col, halo),
         out_shape=out_shape,
         in_specs=in_specs,
-        out_specs=[VSPEC] * len(out_shape),
+        out_specs=[VSPEC] + [ASPEC] * (len(out_shape) - 1),
         scratch_shapes=[
-            pltpu.VMEM((n_row - 1, 8, LANES), F32),
-            pltpu.VMEM((n_col - 1, 8, LANES), F32),
-            pltpu.VMEM((8, LANES), F32),
+            pltpu.VMEM((n_peer, 8, LANES), F32),
             pltpu.SemaphoreType.DMA((n_sem,)),
             pltpu.SemaphoreType.DMA((n_sem,)),
         ],
-        compiler_params=pltpu.CompilerParams(collective_id=1 if halo else 2, has_side_effects=True, vmem_limit_bytes=16 * 1024 * 1024),
+        compiler_params=pltpu.CompilerParams(collective_id=1 if halo else 2, has_side_effects=True, vmem_limit_bytes=VMEM_LIMIT),
         name="exchange",
     )(*args)
 
@@ -276,10 +266,16 @@
     )(x, top, bot, side, tot, norm, add, weights)
 
 
-def proj_kernel(count, per_dev, x_ref, tot_ref, norm_ref, w_ref, out_ref, g, wcat):
+def head_blocks(per_dev):
+    return [(i, min(2, per_dev - i)) for i in range(0, per_dev, 2)]
+
+
+def proj_kernel(count, per_dev, x_ref, tot_ref, norm_ref, w_ref, *refs):
     n_img, n_rows, n_cols, n_chan = x_ref.shape
     per_img = n_rows * n_cols
     hd = w_ref.shape[2]
+    blocks = head_blocks(per_dev)
+    outs, g, wcat = refs[:len(blocks)], refs[-2], refs[-1]
 
     @pl.when(pl.program_id(0) == 0)
     def _():
@@ -289,16 +285,18 @@
         for b in range(n_img):
             z = x_ref[b].reshape(per_img, n_chan).astype(F32)
             g[b * per_img:(b + 1) * per_img, :] = ((z - st[b:b + 1]) * (st[2 + b:3 + b] * gain) + shift).astype(BF16)
-        wcat[per_dev * 3 * hd:, :] = jnp.zeros((wcat.shape[0] - per_dev * 3 * hd, n_chan), BF16)
-
-    for i in range(per_dev):
-        wcat[2 * i * hd:(2 * i + 1) * hd, :] = w_ref[1, i]
-        wcat[(2 * i + 1) * hd:(2 * i + 2) * hd, :] = w_ref[2, i]
-        wcat[(2 * per_dev + i) * hd:(2 * per_dev + i + 1) * hd, :] = w_ref[0, i]
-    for n in range(0, wcat.shape[0], 256):
-        res = lax.dot_general(g[...], wcat[n:n + 256, :], (((1,), (1,)), ((), ())), preferred_element_type=F32).astype(BF16)
+
+    for (first, n), out_ref in zip(blocks, outs):
+        for i in range(n):
+            wcat[2 * i * hd:(2 * i + 1) * hd, :] = w_ref[1, first + i]
+            wcat[(2 * i + 1) * hd:(2 * i + 2) * hd, :] = w_ref[2, first + i]
+            wcat[(2 * n + i) * hd:(2 * n + i + 1) * hd, :] = w_ref[0, first + i]
+        width = out_ref.shape[3]
+        if n == 1:
+            wcat[3 * hd:width, :] = jnp.zeros((width - 3 * hd, n_chan), BF16)
+        res = lax.dot_general(g[...], wcat[0:width, :], (((1,), (1,)), ((), ())), preferred_element_type=F32).astype(BF16)
         for b in range(n_img):
-            out_ref[b, 0, :, n:n + 256] = res[b * per_img:(b + 1) * per_img]
+            out_ref[b, 0] = res[b * per_img:(b + 1) * per_img]
 
 
 def proj(x, tot, norm, weights, n_row, n_col, per_dev):
@@ -306,82 +304,161 @@
     _, n_heads, hd, _ = weights.shape
     count = float(n_rows * n_cols * n_row * n_col * (n_chan // GROUPS))
     n_grp = n_heads // per_dev
-    width = -(-per_dev * 3 * hd // 256) * 256
+    n_tok = n_rows * n_cols
+    widths = [2 * hd * (n + 1) for _, n in head_blocks(per_dev)]
     return pl.pallas_call(
         functools.partial(proj_kernel, count, per_dev),
         grid=(n_grp,),
-        out_shape=jax.ShapeDtypeStruct((n_img, n_grp, n_rows * n_cols, width), BF16),
+        out_shape=[jax.ShapeDtypeStruct((n_img, n_grp, n_tok, w), BF16) for w in widths],
         in_specs=[
             pl.BlockSpec(x.shape, lambda q: (0, 0, 0, 0)),
             pl.BlockSpec((8, LANES), lambda q: (0, 0)),
             pl.BlockSpec(norm.shape, lambda q: (0, 0)),
             pl.BlockSpec((3, per_dev, hd, n_chan), lambda q: (0, q, 0, 0)),
         ],
-        out_specs=pl.BlockSpec((n_img, 1, n_rows * n_cols, width), lambda q: (0, q, 0, 0)),
-        scratch_shapes=[pltpu.VMEM((n_img * n_rows * n_cols, n_chan), BF16), pltpu.VMEM((width, n_chan), BF16)],
+        out_specs=[pl.BlockSpec((n_img, 1, n_tok, w), lambda q: (0, q, 0, 0)) for w in widths],
+        scratch_shapes=[pltpu.VMEM((n_img * n_tok, n_chan), BF16), pltpu.VMEM((max(widths), n_chan), BF16)],
         compiler_params=pltpu.CompilerParams(vmem_limit_bytes=VMEM_LIMIT),
+        cost_estimate=pl.CostEstimate(flops=2 * n_img * n_tok * n_chan * n_grp * sum(widths), bytes_accessed=6 * n_chan * n_chan, transcendentals=0),
         name="proj",
     )(x, tot, norm, weights)
 
 
-def attend_kernel(hd, q_ref, kv_ref, out_ref, qt, vt, ot, qf):
+def attend_kernel(hd, n_pair, q_ref, kv_ref, out_ref, qt, qf, kk, vt, ot, w0, w1, osum, lsum, big):
     n_q, n_k = q_ref.shape[0], kv_ref.shape[0]
-    half = lax.rem(pl.program_id(0), 2)
+    half = pl.multiple_of(pl.program_id(0) * hd, hd)
     factor = 1.4426950408889634 * hd ** -0.5
-    kb, qb = min(1024, n_k), min(512, n_q)
+    kb, qb = w0.shape
     tb = min(512, n_q)
+
+    @pl.when(pl.program_id(0) == 0)
+    def _():
+        lane = lax.broadcasted_iota(jnp.int32, (n_k, 2 * hd), 1)
+        kk[:, 2 * hd:] = jnp.where(lane == 0, 1.0, 0.0).astype(BF16)
+        if n_pair == 1:
+            ot[hd:, :] = jnp.zeros((hd, n_q), F32)
+
+    def flip(t, top):
+        at = pl.multiple_of(t * tb, tb)
+        blk = kv_ref[pl.ds(at, tb), :].astype(F32)
+        turned = blk.T
+        vt[:, pl.ds(at, tb)] = turned[hd:].astype(BF16)
+        lane = lax.broadcasted_iota(jnp.int32, blk.shape, 1)
+        kk[pl.ds(at, tb), 0:2 * hd] = jnp.where(lane < hd, blk, pltpu.roll(blk, hd, 1)).astype(BF16)
+        return jnp.maximum(top, jnp.sum(turned[:hd] * turned[:hd], axis=0, keepdims=True))
+
+    top = lax.fori_loop(0, n_k // tb, flip, jnp.zeros((1, tb), F32))
+    key_norm = jnp.sqrt(jnp.max(top, axis=1, keepdims=True))
+
     for t in range(0, n_q, tb):
         qf[:, t:t + tb] = q_ref[t:t + tb, :].astype(F32).T
-    qt[0:hd, :] = qf[pl.ds(pl.multiple_of(half * hd, hd), hd), :].astype(BF16)
-    qt[hd:, :] = jnp.zeros((qt.shape[0] - hd, n_q), BF16)
-
-    def flip(t, carry):
-        at = pl.multiple_of(t * tb, tb)
-        vt[:, pl.ds(at, tb)] = kv_ref[pl.ds(at, tb), :].astype(F32).T[hd:].astype(BF16)
-        return carry
-
-    lax.fori_loop(0, n_k // tb, flip, 0)
+    scaled = qf[pl.ds(half, hd), :] * factor
+    high = scaled.astype(BF16)
+    qt[0:hd, :] = high
+    qt[hd:2 * hd, :] = (scaled - high.astype(F32)).astype(BF16)
+    bound = jnp.sqrt(jnp.sum(scaled * scaled, axis=0, keepdims=True)) * key_norm
+    row = lax.broadcasted_iota(jnp.int32, (2 * hd, n_q), 0)
+    qt[2 * hd:, :] = jnp.where(row == 0, ROOM - bound, 0.0).astype(BF16)
+
+    n_blk = n_k // kb
 
     def queries(t, carry):
         at = pl.multiple_of(t * qb, qb)
         rhs = qt[:, pl.ds(at, qb)]
 
-        def keys(s, state):
-            run_max, run_sum, out = state
+        def weigh(s, dst):
             pos = pl.multiple_of(s * kb, kb)
-            logits = jnp.dot(kv_ref[pl.ds(pos, kb), :], rhs, preferred_element_type=F32)
-            new_max = jnp.maximum(run_max, jnp.max(logits, axis=0, keepdims=True))
-            scale = jnp.exp2((run_max - new_max) * factor)
-            w = jnp.exp2((logits - new_max) * factor)
-            run_sum = run_sum * scale + jnp.sum(w, axis=0, keepdims=True)
-            out = out * scale + jnp.dot(vt[:, pl.ds(pos, kb)], w.astype(BF16), preferred_element_type=F32)
-            return new_max, run_sum, out
-
-        init = (jnp.full((1, qb), -jnp.inf, F32), jnp.zeros((1, qb), F32), jnp.zeros((hd, qb), F32))
-        _, run_sum, out = lax.fori_loop(0, n_k // kb, keys, init)
-        ot[pl.ds(pl.multiple_of(half * hd, hd), hd), pl.ds(at, qb)] = out / run_sum
+            w = jnp.exp2(jnp.dot(kk[pl.ds(pos, kb), :], rhs, preferred_element_type=F32))
+            dst[...] = w.astype(BF16)
+            return jnp.sum(w.reshape(kb // 8, 8, qb), axis=0)
+
+        def gather(s, src):
+            pos = pl.multiple_of(s * kb, kb)
+            osum[...] += jnp.dot(vt[:, pl.ds(pos, kb)], src[...], preferred_element_type=F32)
+
+        osum[...] = jnp.zeros_like(osum)
+        total = weigh(0, w0)
+
+        def keys(j, total):
+            total += weigh(2 * j + 1, w1)
+            gather(2 * j, w0)
+            total += weigh(2 * j + 2, w0)
+            gather(2 * j + 1, w1)
+            return total
+
+        total = lax.fori_loop(0, n_blk // 2 - 1, keys, total)
+        total += weigh(n_blk - 1, w1)
+        gather(n_blk - 2, w0)
+        gather(n_blk - 1, w1)
+        total = jnp.sum(total, axis=0, keepdims=True)
+        lsum[:, pl.ds(at, qb)] = total
+        big[:, pl.ds(at, qb)] = jnp.max(jnp.abs(osum[...]), axis=0, keepdims=True)
+        ot[pl.ds(half, hd), pl.ds(at, qb)] = osum[...] / total
         return carry
 
     lax.fori_loop(0, n_q // qb, queries, 0)
+    sound = (jnp.min(lsum[...]) >= TINY) & (jnp.max(big[...]) <= 3e38) & (jnp.max(lsum[...]) <= 3e38)
+
+    @pl.when(jnp.logical_not(sound))
+    def _():
+        qt[2 * hd:, :] = jnp.zeros((2 * hd, n_q), BF16)
+        sk, sq = min(256, n_k), min(256, n_q)
+
+        def some_queries(t, carry):
+            at = pl.multiple_of(t * sq, sq)
+
+            def some_keys(s, state):
+                run_max, run_sum, out = state
+                pos = pl.multiple_of(s * sk, sk)
+                logits = jnp.dot(kk[pl.ds(pos, sk), :], qt[:, pl.ds(at, sq)], preferred_element_type=F32)
+                new_max = jnp.maximum(run_max, jnp.max(logits, axis=0, keepdims=True))
+                scale = jnp.exp2(run_max - new_max)
+                w = jnp.exp2(logits - new_max)
+                run_sum = run_sum * scale + jnp.sum(w, axis=0, keepdims=True)
+                out = out * scale + jnp.dot(vt[:, pl.ds(pos, sk)], w.astype(BF16), preferred_element_type=F32)
+                return new_max, run_sum, out
+
+            init = (jnp.full((1, sq), -jnp.inf, F32), jnp.zeros((1, sq), F32), jnp.zeros((hd, sq), F32))
+            _, run_sum, out = lax.fori_loop(0, n_k // sk, some_keys, init)
+            ot[pl.ds(half, hd), pl.ds(at, sq)] = out / run_sum
+            return carry
+
+        lax.fori_loop(0, n_q // sq, some_queries, 0)
+
     for t in range(0, n_q, tb):
         out_ref[t:t + tb, :] = ot[:, t:t + tb].T.astype(BF16)
 
 
-def attend(q, kv, hd, per_dev):
+def attend(q, kv, hd, n_pair, kb=1024, qb=768):
     n_q, n_k = q.shape[0], kv.shape[0]
+    kb, qb = min(kb, n_k // 2), min(qb, n_q)
     return pl.pallas_call(
-        functools.partial(attend_kernel, hd),
-        grid=(per_dev,),
+        functools.partial(attend_kernel, hd, n_pair),
+        grid=(n_pair,),
         out_shape=jax.ShapeDtypeStruct(q.shape, BF16),
-        in_specs=[pl.BlockSpec((n_q, 2 * hd), lambda i: (0, i // 2)), pl.BlockSpec((n_k, 2 * hd), lambda i: (0, i))],
-        out_specs=pl.BlockSpec((n_q, 2 * hd), lambda i: (0, i // 2)),
-        scratch_shapes=[pltpu.VMEM((2 * hd, n_q), BF16), pltpu.VMEM((hd, n_k), BF16), pltpu.VMEM((2 * hd, n_q), F32), pltpu.VMEM((2 * hd, n_q), F32)],
+        in_specs=[pl.BlockSpec((n_q, 2 * hd), lambda i: (0, 0)), pl.BlockSpec((n_k, 2 * hd), lambda i: (0, i))],
+        out_specs=pl.BlockSpec((n_q, 2 * hd), lambda i: (0, 0)),
+        scratch_shapes=[
+            pltpu.VMEM((4 * hd, n_q), BF16),
+            pltpu.VMEM((2 * hd, n_q), F32),
+            pltpu.VMEM((n_k, 4 * hd), BF16),
+            pltpu.VMEM((hd, n_k), BF16),
+            pltpu.VMEM((2 * hd, n_q), F32),
+            pltpu.VMEM((kb, qb), BF16),
+            pltpu.VMEM((kb, qb), BF16),
+            pltpu.VMEM((hd, qb), F32),
+            pltpu.VMEM((1, n_q), F32),
+            pltpu.VMEM((1, n_q), F32),
+        ],
         compiler_params=pltpu.CompilerParams(vmem_limit_bytes=VMEM_LIMIT),
+        cost_estimate=pl.CostEstimate(flops=16 * n_pair * n_q * n_k * hd, bytes_accessed=n_pair * n_k * hd * 4, transcendentals=n_pair * n_q * n_k),
         name="attend",
     )(q, kv)
 
 
-def outproj_kernel(o_ref, w_ref, x_ref, out_ref, edge_ref, part_ref, wcat, acc, csum):
+def outproj_kernel(n_in, *refs):
+    o_refs = refs[:n_in]
+    w_ref, x_ref, out_ref, edge_ref, part_ref, wcat, acc, csum = refs[n_in:]
     n_img, n_rows, n_cols, n_chan = x_ref.shape
     per_dev, hd, _ = w_ref.shape[1:]
     per_img = n_rows * n_cols
@@ -394,7 +471,7 @@
 
     for i in range(per_dev):
         wcat[i * hd:(i + 1) * hd, :] = w_ref[0, i]
-    lhs = o_ref[:, 0].reshape(n_img * per_img, o_ref.shape[3])
+    lhs = jnp.concatenate([o[:, 0].reshape(n_img * per_img, o.shape[3]) for o in o_refs], axis=1)
     for n in range(0, n_chan, 256):
         acc[:, n:n + 256] += jnp.dot(lhs, wcat[:, n:n + 256], preferred_element_type=F32)
 
@@ -403,24 +480,24 @@
         finish(acc, out_ref, edge_ref, part_ref, csum)
 
 
-def outproj(o, weights, x, per_dev):
-    n_img, n_grp, n_tok, width = o.shape
+def outproj(outs, weights, x, per_dev):
+    n_img, n_grp, n_tok, width = outs[0].shape
     _, n_heads, hd, n_chan = weights.shape
     shapes = [jax.ShapeDtypeStruct(x.shape, BF16)] + finish_shapes(x.shape)
     return pl.pallas_call(
-        outproj_kernel,
+        functools.partial(outproj_kernel, len(outs)),
         grid=(n_grp,),
         out_shape=shapes,
-        in_specs=[
-            pl.BlockSpec((n_img, 1, n_tok, width), lambda q: (0, q, 0, 0)),
+        in_specs=[pl.BlockSpec((n_img, 1, n_tok, width), lambda q: (0, q, 0, 0)) for _ in outs] + [
             pl.BlockSpec((1, per_dev, hd, n_chan), lambda q: (3, q, 0, 0)),
             pl.BlockSpec(x.shape, lambda q: (0, 0, 0, 0)),
         ],
         out_specs=[pl.BlockSpec(s.shape, lambda q, n=len(s.shape): (0,) * n) for s in shapes],
-        scratch_shapes=[pltpu.VMEM((width, n_chan), BF16), pltpu.VMEM((n_img * n_tok, n_chan), F32), pltpu.VMEM((8, n_chan), F32)],
+        scratch_shapes=[pltpu.VMEM((len(outs) * width, n_chan), BF16), pltpu.VMEM((n_img * n_tok, n_chan), F32), pltpu.VMEM((8, n_chan), F32)],
         compiler_params=pltpu.CompilerParams(vmem_limit_bytes=VMEM_LIMIT),
+        cost_estimate=pl.CostEstimate(flops=2 * n_img * n_tok * n_chan * n_chan, bytes_accessed=2 * n_chan * n_chan, transcendentals=0),
         name="outproj",
-    )(o, weights, x)
+    )(*outs, weights, x)
 
 
 def solution(mesh):
@@ -442,13 +519,17 @@
         n_tok = n_rows * n_cols
         tot, = exchange(part, n_row, n_col)
         qkv = proj(x, tot, norm, weights, n_row, n_col, per_dev)
-        qkv = lax.all_to_all(qkv.reshape(n_row, n_tok, -1), 'row', 0, 0).reshape(n_row * n_tok, -1)
-        kv_width = per_dev * 2 * hd
-        q_width = -(-per_dev // 2) * 2 * hd
-        kv = lax.all_gather(qkv[:, :kv_width], 'col', axis=0, tiled=True)
-        out = attend(qkv[:, kv_width:kv_width + q_width], kv, hd, per_dev)
-        out = lax.all_to_all(out.reshape(n_row, n_tok, q_width), 'row', 0, 0)
-        return outproj(out.reshape(n_img, -1, n_tok, q_width), weights, x, per_dev)
+        blocks = head_blocks(per_dev)
+        outs = [None] * len(blocks)
+        for k in sorted(range(len(blocks)), key=lambda k: blocks[k][1]):
+            n_pair = blocks[k][1]
+            kv_width = n_pair * 2 * hd
+            mine = lax.all_to_all(qkv[k].reshape(n_row, n_tok, -1), 'row', 0, 0).reshape(n_row * n_tok, -1)
+            kv = lax.all_gather(mine[:, :kv_width], 'col', axis=0, tiled=True)
+            out = attend(mine[:, kv_width:], kv, hd, n_pair)
+            out = lax.all_to_all(out.reshape(n_row, n_tok, 2 * hd), 'row', 0, 0)
+            outs[k] = out.reshape(n_img, -1, n_tok, 2 * hd)
+        return outproj(outs, weights, x, per_dev)
 
     def run_stage(latent, t_emb, res_norm, res_conv, res_temb, attn_norm, attn_proj):
         edge, part = prep(latent)

time: 430 us -> 339 us (0.79)
  waiting for transfers between devices: 87.2 us -> 10 us
  local copies, waits for them, and re-layouts: 26.2 us -> 5.12 us
  Pallas kernels: 248 us -> 229 us
  blocking collectives: 42.1 us -> 55.9 us
  starting transfers between devices: 5.19 us -> 14.8 us
    all_gather x1 -> x3, waiting for transfers between devices: 74 us -> 5.42 us  [attn_block(): kv = lax.all_gather(mine[:, :kv_width], 'col', axis=0, tiled=True)]
    pallas_call x2 -> x4, Pallas kernels: 109 us -> 74 us  [the longest x3 66.9 us: attend(): pl.pallas_call(functools.partial(attend_kernel, hd, n_pair), grid=(n_pair...]
    unnamed x64 -> x12, local copies, waits for them, and re-layouts: 23.4 us -> 0.76 us
    pallas_call x5, Pallas kernels: 51.2 us -> 66 us  [exchange(): pl.pallas_call(functools.partial(exchange_kernel, n_row, n_col, halo), ou...]
    all_to_all x1 -> x3, blocking collectives: 42.1 us -> 55.9 us  [attn_block(): lax.all_to_all(qkv[k].reshape(n_row, n_tok, -1), 'row', 0, 0)]
    all_to_all x1 -> x3, starting transfers between devices: 5.19 us -> 14.7 us  [attn_block(): out = lax.all_to_all(out.reshape(n_row, n_tok, 2 * hd), 'row', 0, 0)]
    all_to_all x1 -> x3, waiting for transfers between devices: 13.1 us -> 4.46 us  [attn_block(): out = lax.all_to_all(out.reshape(n_row, n_tok, 2 * hd), 'row', 0, 0)]
  transfers between devices with their start and end apart: 2 -> 6, of which waited for: 2 -> 2; matrix products, arithmetic and copies ran while one was open for 1% -> 2% of each run, Pallas kernels for 0% -> 20%
where the time goes in v2:
time: 339 us; the launch traced here: 335 us
  Pallas kernels  229 us (68%)
  blocking collectives  55.9 us (16%)
  starting transfers between devices  14.8 us (4%)
  between operations  13.6 us (4%)
  waiting for transfers between devices  10 us (3%)
  matrix products  6.17 us (2%)
  local copies, waits for them, and re-layouts  5.12 us (2%)
    pallas_call x4, Pallas kernels, conv(): pl.pallas_call(functools.partial(conv_kernel, blk, idx, n_row, n_col, cou...  76.2 us
    pallas_call x3, Pallas kernels, attend(): pl.pallas_call(functools.partial(attend_kernel, hd, n_pair), grid=(n_pair...  66.9 us
    pallas_call x5, Pallas kernels, exchange(): pl.pallas_call(functools.partial(exchange_kernel, n_row, n_col, halo), ou...  66 us
    all_to_all x3, blocking collectives, attn_block(): lax.all_to_all(qkv[k].reshape(n_row, n_tok, -1), 'row', 0, 0)  55.9 us
    all_to_all x3, starting transfers between devices, attn_block(): out = lax.all_to_all(out.reshape(n_row, n_tok, 2 * hd), 'row', 0, 0)  14.7 us
    pallas_call x1, Pallas kernels, proj(): pl.pallas_call(functools.partial(proj_kernel, count, per_dev), grid=(n_gr...  10.3 us
    pallas_call x1, Pallas kernels, outproj(): pl.pallas_call(functools.partial(outproj_kernel, len(outs)), grid=(n_grp,...  7.13 us
  transfers between devices with their start and end apart: 6, of which 2 were waited for; matrix products, arithmetic and copies ran while one was open for 2% of the time, Pallas kernels for 20%

profile of v2, /device:TPU:97, one launch (start us, length us, event | category | flops | bytes accessed | tf_op | source)
XLA Modules:
  0.0 334.8 jit_solution(5062373345378305434)
XLA Ops:
  6.5 0.0 all-gather.8.cloned.1.call-start
  6.6 2.7 prep.1
  9.2 3.1 fusion.2.add_ref
  12.3 16.8 %exchange.5 = (f32[8,128]{1,0:T(8,128)}, bf16[2,48,1280]{2,1,0:T(8,128)(2,1)}, bf16[2,48,1280]{2,1,0:T(8,128)(2,1)}, bf16[2,6,2,1280]{3,2,1,0:T(2,128)(2,1)}) custom-call(f32[8,128]{1,0:T(8,128)} %get-tuple-element.38.refs_0_, bf16[2,4,48,1280]{3,2,1,0:T(8,128)(2,1)} %add_ref.1, bf16[2,4,2,1280]{3,2,1,0:T(2,128)(2,1)} %get-tuple-element.39.refs_2_), custom_call_target="tpu_custom_call" | custom-call | tf_op jit(solution)/shard_map/exchange/pallas_call | solution.py:155
  29.1 18.8 %conv.4 = (bf16[2,4,48,1280]{3,2,1,0:T(8,128)(2,1)}, bf16[2,4,2,1280]{3,2,1,0:T(2,128)(2,1)}, f32[8,128]{1,0:T(8,128)}) custom-call(bf16[2,4,48,1280]{3,2,1,0:T(8,128)(2,1)} %add_ref.1, bf16[2,48,1280]{2,1,0:T(8,128)(2,1)} %get-tuple-element.40.top_ref, bf16[2,48,1280]{2,1,0:T(8,128)(2,1)} %get-tuple-element.41.bot_ref, ...), custom_call_target="tpu_custom_call" | custom-call | flops 11324620800 | bytes 29491200 | tf_op jit(solution)/shard_map/conv/pallas_call | solution.py:249
  48.0 12.4 %exchange.6 = (f32[8,128]{1,0:T(8,128)}, bf16[2,48,1280]{2,1,0:T(8,128)(2,1)}, bf16[2,48,1280]{2,1,0:T(8,128)(2,1)}, bf16[2,6,2,1280]{3,2,1,0:T(2,128)(2,1)}) custom-call(f32[8,128]{1,0:T(8,128)} %get-tuple-element.45.refs_0_, bf16[2,4,48,1280]{3,2,1,0:T(8,128)(2,1)} %get-tuple-element.44.refs_1_.x_ref, bf16[2,4,2,1280]{3,2,1,0:T(2,128)(2,1)} %get-tuple-element.46.refs_2_), custom_call_target="tpu_custom_call" | custom-call | tf_op jit(solution)/shard_map/exchange/pallas_call | solution.py:155
  60.4 19.3 %conv.5 = (bf16[2,4,48,1280]{3,2,1,0:T(8,128)(2,1)}, bf16[2,4,2,1280]{3,2,1,0:T(2,128)(2,1)}, f32[8,128]{1,0:T(8,128)}) custom-call(bf16[2,4,48,1280]{3,2,1,0:T(8,128)(2,1)} %get-tuple-element.44.refs_1_.x_ref, bf16[2,48,1280]{2,1,0:T(8,128)(2,1)} %get-tuple-element.47.top_ref, bf16[2,48,1280]{2,1,0:T(8,128)(2,1)} %get-tuple-element.48.bot_ref, ...), custom_call_target="tpu_custom_call" | custom-call | flops 11324620800 | bytes 29491200 | tf_op jit(solution)/shard_map/conv/pallas_call | solution.py:249
  79.8 11.6 %exchange.7.tot_ref = f32[8,128]{1,0:T(8,128)} custom-call(f32[8,128]{1,0:T(8,128)} %get-tuple-element.52.refs_0_), custom_call_target="tpu_custom_call" | custom-call | tf_op jit(solution)/shard_map/exchange/pallas_call | solution.py:155
  91.3 10.3 %proj.1 = (bf16[2,4,192,384]{3,2,1,0:T(8,128)(2,1)}, bf16[2,4,192,384]{3,2,1,0:T(8,128)(2,1)}, bf16[2,4,192,256]{3,2,1,0:T(8,128)(2,1)}) custom-call(bf16[2,4,48,1280]{3,2,1,0:T(8,128)(2,1)} %get-tuple-element.51.x_ref.refs_4_, f32[8,128]{1,0:T(8,128)} %exchange.7.tot_ref, bf16[2,1280]{1,0:T(2,128)(2,1)} %norm_ref.7, bf16[4,20,64,1280]{3,2,1,0:T(8,128)(2,1)} %bitcast.19), custom_call_target="tpu_custom_call" | custom-call | flops 4026531840 | bytes 9830400 | tf_op jit(solution)/shard_map/proj/pallas_call | solution.py:309
  101.6 0.0 copy-start.4
  101.6 16.0 %all_to_all.30 = bf16[8,192,256]{2,1,0:T(8,128)(2,1)S(1)} all-to-all(bf16[8,192,256]{2,1,0:T(8,128)(2,1)} %bitcast.31), channel_id=1, replica_groups=mesh['dp'=1,'col'=4,'row'=8] {'row'}, dimensions={0} | all-to-all | bytes 1572864 | tf_op jit(solution)/shard_map/all_to_all | solution.py:527
  117.6 0.0 copy-start.3
  117.6 0.9 fusion.11
  118.5 0.1 all-gather.8.cloned.1.call-update
  118.6 0.1 all-gather.4.cloned.1.call-start
  118.7 0.0 copy-done.4
  118.7 20.1 %all_to_all.31 = bf16[8,192,384]{2,1,0:T(8,128)(2,1)S(1)} all-to-all(bf16[8,192,384]{2,1,0:T(8,128)(2,1)S(1)} %bitcast.30), channel_id=1, replica_groups=mesh['dp'=1,'col'=4,'row'=8] {'row'}, dimensions={0} | all-to-all | bytes 2359296 | tf_op jit(solution)/shard_map/all_to_all | solution.py:527
  138.8 0.9 slice.33
  139.7 0.1 all-gather.4.cloned.1.call-update
  139.8 0.1 all-gather.6.cloned.1.call-start
  139.9 0.0 copy-done.3
  139.9 19.8 %all_to_all.32 = bf16[8,192,384]{2,1,0:T(8,128)(2,1)S(1)} all-to-all(bf16[8,192,384]{2,1,0:T(8,128)(2,1)S(1)} %bitcast.29), channel_id=1, replica_groups=mesh['dp'=1,'col'=4,'row'=8] {'row'}, dimensions={0} | all-to-all | bytes 2359296 | tf_op jit(solution)/shard_map/all_to_all | solution.py:527
  159.7 1.0 slice.35
  160.6 0.1 all-gather.6.cloned.1.call-update
  160.7 0.8 slice.32.q_ref
  161.5 0.8 slice.34.q_ref
  162.2 0.0 all-gather.8.cloned.1.call-done.kv_ref
  162.2 14.3 %attend.5 = bf16[1536,128]{1,0:T(8,128)(2,1)} custom-call(bf16[1536,128]{1,0:T(8,128)(2,1)} %get-tuple-element.72.q_ref, bf16[6144,128]{1,0:T(8,128)(2,1)} %all-gather.8.cloned.1.call-done.kv_ref), custom_call_target="tpu_custom_call" | custom-call | flops 9663676416 | bytes 1572864 | tf_op jit(solution)/shard_map/attend/pallas_call | solution.py:435
  176.5 4.2 %all-to-all-start.5 = ((bf16[8,192,128]{2,1,0:T(8,128)(2,1)}), bf16[8,192,128]{2,1,0:T(8,128)(2,1)S(1)}, u32[]{:S(2)}, u32[]{:S(2)}) async-start(bf16[8,192,128]{2,1,0:T(8,128)(2,1)} %bitcast.33), calls=%async_computation.5 | async-start | bytes 786432 | tf_op jit(solution)/shard_map/all_to_all | solution.py:530
  180.8 26.3 %attend.3 = bf16[1536,128]{1,0:T(8,128)(2,1)} custom-call(bf16[1536,128]{1,0:T(8,128)(2,1)} %slice.32.q_ref, bf16[6144,256]{1,0:T(8,128)(2,1)} %all-gather.4.cloned.1.call-done.kv_ref), custom_call_target="tpu_custom_call" | custom-call | flops 19327352832 | bytes 3145728 | tf_op jit(solution)/shard_map/attend/pallas_call | solution.py:435
  207.1 0.0 all-to-all-done.5
  207.1 5.2 %all-to-all-start.1 = ((bf16[8,192,128]{2,1,0:T(8,128)(2,1)}), bf16[8,192,128]{2,1,0:T(8,128)(2,1)S(1)}, u32[]{:S(2)}, u32[]{:S(2)}) async-start(bf16[8,192,128]{2,1,0:T(8,128)(2,1)} %bitcast.32), calls=%async_computation.1 | async-start | bytes 786432 | tf_op jit(solution)/shard_map/all_to_all | solution.py:530
  212.3 0.0 copy-start.5
  212.3 5.4 %all-gather.6.cloned.1.call-done.kv_ref = bf16[6144,256]{1,0:T(8,128)(2,1)} async-done(((bf16[1536,256]{1,0:T(8,128)(2,1)}), bf16[6144,256]{1,0:T(8,128)(2,1)}) %all-gather.6.cloned.1.call-update) | async-done | bytes 3145744 | tf_op jit(solution)/shard_map/all_gather | solution.py:528
  217.7 26.3 %attend.4 = bf16[1536,128]{1,0:T(8,128)(2,1)} custom-call(bf16[1536,128]{1,0:T(8,128)(2,1)} %slice.34.q_ref, bf16[6144,256]{1,0:T(8,128)(2,1)} %all-gather.6.cloned.1.call-done.kv_ref), custom_call_target="tpu_custom_call" | custom-call | flops 19327352832 | bytes 3145728 | tf_op jit(solution)/shard_map/attend/pallas_call | solution.py:435
  244.1 0.0 copy-done
  244.1 0.0 all-to-all-done.1
  244.1 5.2 %all-to-all-start.3 = ((bf16[8,192,128]{2,1,0:T(8,128)(2,1)}), bf16[8,192,128]{2,1,0:T(8,128)(2,1)S(1)}, u32[]{:S(2)}, u32[]{:S(2)}) async-start(bf16[8,192,128]{2,1,0:T(8,128)(2,1)} %bitcast.34), calls=%async_computation.3 | async-start | bytes 786432 | tf_op jit(solution)/shard_map/all_to_all | solution.py:530
  249.3 0.0 copy-done.5
  249.3 3.1 fusion.add_ref
  252.4 4.5 %all-to-all-done.3 = bf16[8,192,128]{2,1,0:T(8,128)(2,1)S(1)} async-done(((bf16[8,192,128]{2,1,0:T(8,128)(2,1)}), bf16[8,192,128]{2,1,0:T(8,128)(2,1)S(1)}, u32[]{:S(2)}, u32[]{:S(2)}) %all-to-all-start.3) | async-done | bytes 393248 | tf_op jit(solution)/shard_map/all_to_all | solution.py:530
  256.8 0.0 copy-done.1
  256.8 0.7 copy-done.2
  257.6 7.1 %outproj.1 = (bf16[2,4,48,1280]{3,2,1,0:T(8,128)(2,1)}, bf16[2,4,2,1280]{3,2,1,0:T(2,128)(2,1)}, f32[8,128]{1,0:T(8,128)}) custom-call(bf16[2,4,192,128]{3,2,1,0:T(8,128)(2,1)} %bitcast.27, bf16[2,4,192,128]{3,2,1,0:T(8,128)(2,1)} %bitcast.28, bf16[2,4,192,128]{3,2,1,0:T(8,128)(2,1)} %bitcast.26, bf16[4,20,64,1280]{3,2,1,0:T(8,128)(2,1)} %bitcast.20, ...), custom_call_target="tpu_custom_call" | custom-call | flops 1258291200 | bytes 3276800 | tf_op jit(solution)/shard_map/outproj/pallas_call | solution.py:487
  264.7 12.7 %exchange.8 = (f32[8,128]{1,0:T(8,128)}, bf16[2,48,1280]{2,1,0:T(8,128)(2,1)}, bf16[2,48,1280]{2,1,0:T(8,128)(2,1)}, bf16[2,6,2,1280]{3,2,1,0:T(2,128)(2,1)}) custom-call(f32[8,128]{1,0:T(8,128)} %get-tuple-element.57.refs_0_, bf16[2,4,48,1280]{3,2,1,0:T(8,128)(2,1)} %get-tuple-element.56.refs_1_.x_ref.add_ref, bf16[2,4,2,1280]{3,2,1,0:T(2,128)(2,1)} %get-tuple-element.58.refs_2_), custom_call_target="tpu_custom_call" | custom-call | tf_op jit(solution)/shard_map/exchange/pallas_call | solution.py:155
  277.4 18.8 %conv.6 = (bf16[2,4,48,1280]{3,2,1,0:T(8,128)(2,1)}, bf16[2,4,2,1280]{3,2,1,0:T(2,128)(2,1)}, f32[8,128]{1,0:T(8,128)}) custom-call(bf16[2,4,48,1280]{3,2,1,0:T(8,128)(2,1)} %get-tuple-element.56.refs_1_.x_ref.add_ref, bf16[2,48,1280]{2,1,0:T(8,128)(2,1)} %get-tuple-element.59.top_ref, bf16[2,48,1280]{2,1,0:T(8,128)(2,1)} %get-tuple-element.60.bot_ref, ...), custom_call_target="tpu_custom_call" | custom-call | flops 11324620800 | bytes 29491200 | tf_op jit(solution)/shard_map/conv/pallas_call | solution.py:249
  296.2 12.5 %exchange.9 = (f32[8,128]{1,0:T(8,128)}, bf16[2,48,1280]{2,1,0:T(8,128)(2,1)}, bf16[2,48,1280]{2,1,0:T(8,128)(2,1)}, bf16[2,6,2,1280]{3,2,1,0:T(2,128)(2,1)}) custom-call(f32[8,128]{1,0:T(8,128)} %get-tuple-element.64.refs_0_, bf16[2,4,48,1280]{3,2,1,0:T(8,128)(2,1)} %get-tuple-element.63.refs_1_.x_ref, bf16[2,4,2,1280]{3,2,1,0:T(2,128)(2,1)} %get-tuple-element.65.refs_2_), custom_call_target="tpu_custom_call" | custom-call | tf_op jit(solution)/shard_map/exchange/pallas_call | solution.py:155
  308.8 19.2 %conv.7 = (bf16[2,4,48,1280]{3,2,1,0:T(8,128)(2,1)}, bf16[2,4,2,1280]{3,2,1,0:T(2,128)(2,1)}, f32[8,128]{1,0:T(8,128)}) custom-call(bf16[2,4,48,1280]{3,2,1,0:T(8,128)(2,1)} %get-tuple-element.63.refs_1_.x_ref, bf16[2,48,1280]{2,1,0:T(8,128)(2,1)} %get-tuple-element.66.top_ref, bf16[2,48,1280]{2,1,0:T(8,128)(2,1)} %get-tuple-element.67.bot_ref, ...), custom_call_target="tpu_custom_call" | custom-call | flops 11324620800 | bytes 29491200 | tf_op jit(solution)/shard_map/conv/pallas_call | solution.py:249
  (4 shorter events, 0.0 us)
Async XLA Ops:
  6.5 155.7 %all-gather.8.cloned.1.call-start = ((), (), s32[]{:S(2)}) async-start(), calls=%async_computation.8 | async-start | bytes 1966080 | tf_op jit(solution)/shard_map/all_gather | solution.py:528
  101.6 17.1 %copy-start.4 = (bf16[2,4,192,384]{3,2,1,0:T(8,128)(2,1)S(1)}, bf16[2,4,192,384]{3,2,1,0:T(8,128)(2,1)}, u32[]{:S(2)}) copy-start(bf16[2,4,192,384]{3,2,1,0:T(8,128)(2,1)} %get-tuple-element.53) | copy-start | bytes 3538948
  117.6 22.3 %copy-start.3 = (bf16[2,4,192,384]{3,2,1,0:T(8,128)(2,1)S(1)}, bf16[2,4,192,384]{3,2,1,0:T(8,128)(2,1)}, u32[]{:S(2)}) copy-start(bf16[2,4,192,384]{3,2,1,0:T(8,128)(2,1)} %get-tuple-element.54) | copy-start | bytes 3538948
  118.6 62.2 %all-gather.4.cloned.1.call-start = ((), (), s32[]{:S(2)}) async-start(), calls=%async_computation.6 | async-start | bytes 3932160 | tf_op jit(solution)/shard_map/all_gather | solution.py:528
  139.8 78.0 %all-gather.6.cloned.1.call-start = ((), (), s32[]{:S(2)}) async-start(), calls=%async_computation.7 | async-start | bytes 3932160 | tf_op jit(solution)/shard_map/all_gather | solution.py:528
  176.5 30.5 %all-to-all-start.5 = ((bf16[8,192,128]{2,1,0:T(8,128)(2,1)}), bf16[8,192,128]{2,1,0:T(8,128)(2,1)S(1)}, u32[]{:S(2)}, u32[]{:S(2)}) async-start(bf16[8,192,128]{2,1,0:T(8,128)(2,1)} %bitcast.33), calls=%async_computation.5 | async-start | bytes 786432 | tf_op jit(solution)/shard_map/all_to_all | solution.py:530
  207.1 37.0 %copy-start = (bf16[8,192,128]{2,1,0:T(8,128)(2,1)}, bf16[8,192,128]{2,1,0:T(8,128)(2,1)S(1)}, u32[]{:S(2)}) copy-start(bf16[8,192,128]{2,1,0:T(8,128)(2,1)S(1)} %all-to-all-done.5) | copy-start | bytes 1179652
  207.1 37.0 %all-to-all-start.1 = ((bf16[8,192,128]{2,1,0:T(8,128)(2,1)}), bf16[8,192,128]{2,1,0:T(8,128)(2,1)S(1)}, u32[]{:S(2)}, u32[]{:S(2)}) async-start(bf16[8,192,128]{2,1,0:T(8,128)(2,1)} %bitcast.32), calls=%async_computation.1 | async-start | bytes 786432 | tf_op jit(solution)/shard_map/all_to_all | solution.py:530
  212.3 37.0 %copy-start.5 = (bf16[2,1280]{1,0:T(2,128)(2,1)S(1)}, bf16[2,1280]{1,0:T(2,128)(2,1)}, u32[]{:S(2)}) copy-start(bf16[2,1280]{1,0:T(2,128)(2,1)} %param.8) | copy-start | bytes 15364
  244.1 12.8 %copy-start.1 = (bf16[8,192,128]{2,1,0:T(8,128)(2,1)}, bf16[8,192,128]{2,1,0:T(8,128)(2,1)S(1)}, u32[]{:S(2)}) copy-start(bf16[8,192,128]{2,1,0:T(8,128)(2,1)S(1)} %all-to-all-done.1) | copy-start | bytes 1179652
  244.1 12.7 %all-to-all-start.3 = ((bf16[8,192,128]{2,1,0:T(8,128)(2,1)}), bf16[8,192,128]{2,1,0:T(8,128)(2,1)S(1)}, u32[]{:S(2)}, u32[]{:S(2)}) async-start(bf16[8,192,128]{2,1,0:T(8,128)(2,1)} %bitcast.34), calls=%async_computation.3 | async-start | bytes 786432 | tf_op jit(solution)/shard_map/all_to_all | solution.py:530
  256.8 0.7 copy-start.2
Sparse Core Ops, SparseCore 0:
  118.7 21.9 all-gather.7
  142.3 36.8 all-gather.3
  180.7 36.9 all-gather.5

commit v3 on v2

--- a/solution.py
+++ b/solution.py
@@ -64,10 +64,19 @@
     part_ref[...] = jnp.dot(csum[...], group_mask(n_chan, 0), precision=HIGH, preferred_element_type=F32)
 
 
-def prep_kernel(x_ref, edge_ref, part_ref, acc, dump, csum):
-    n_img, n_rows, n_cols, n_chan = x_ref.shape
+def prep_kernel(x_ref, emb_ref, w_hbm, edge_ref, part_ref, t_ref, acc, dump, csum, wbuf, sem):
+    n_blk = w_hbm.shape[0]
+    loads = [pltpu.make_async_copy(w_hbm.at[k], wbuf.at[k], sem.at[k]) for k in range(n_blk)]
+    for cp in loads:
+        cp.start()
     acc[...] = x_ref[...].reshape(acc.shape).astype(F32)
     finish(acc, dump, edge_ref, part_ref, csum)
+    emb = silu(emb_ref[...].astype(F32))
+    n_img = emb.shape[0]
+    emb = jnp.concatenate([emb, jnp.zeros((8 - n_img, emb.shape[1]), F32)], axis=0).astype(BF16)
+    for k, cp in enumerate(loads):
+        cp.wait()
+        t_ref[k] = jnp.dot(emb, wbuf[k], preferred_element_type=F32)[0:n_img]
 
 
 def finish_shapes(shape):
@@ -75,28 +84,37 @@
     return [jax.ShapeDtypeStruct((2, n_rows, n_img, n_chan), BF16), jax.ShapeDtypeStruct((8, LANES), F32)]
 
 
-def prep(x):
-    n_tok = x.shape[0] * x.shape[1] * x.shape[2]
+def prep(x, t_emb, w_temb):
+    n_img, n_rows, n_cols, n_chan = x.shape
     return pl.pallas_call(
         prep_kernel,
-        out_shape=finish_shapes(x.shape),
-        in_specs=[VSPEC],
-        out_specs=[VSPEC, VSPEC],
-        scratch_shapes=[pltpu.VMEM((n_tok, x.shape[3]), F32), pltpu.VMEM(x.shape, BF16), pltpu.VMEM((8, x.shape[3]), F32)],
+        out_shape=finish_shapes(x.shape) + [jax.ShapeDtypeStruct((w_temb.shape[0], n_img, n_chan), F32)],
+        in_specs=[VSPEC, VSPEC, ASPEC],
+        out_specs=[VSPEC, VSPEC, VSPEC],
+        scratch_shapes=[
+            pltpu.VMEM((n_img * n_rows * n_cols, n_chan), F32),
+            pltpu.VMEM(x.shape, BF16),
+            pltpu.VMEM((8, n_chan), F32),
+            pltpu.VMEM(w_temb.shape, BF16),
+            pltpu.SemaphoreType.DMA((w_temb.shape[0],)),
+        ],
         compiler_params=pltpu.CompilerParams(vmem_limit_bytes=VMEM_LIMIT),
         name="prep",
-    )(x)
+    )(x, t_emb, w_temb)
 
 
 def exchange_kernel(n_row, n_col, halo, *refs):
     if halo:
-        part_ref, x_ref, edge_ref, tot_ref, top_ref, bot_ref, side_ref, buf, send, recv = refs
+        part_ref, x_ref, edge_ref, tot_ref, top_ref, bot_ref, side_ref, rbuf, cbuf, rsum, send, recv = refs
     else:
-        part_ref, tot_ref, buf, send, recv = refs
+        part_ref, tot_ref, rbuf, cbuf, rsum, send, recv = refs
     r, c = lax.axis_index('row'), lax.axis_index('col')
     up, down = lax.rem(r + n_row - 1, n_row), lax.rem(r + 1, n_row)
     left, right = lax.rem(c + n_col - 1, n_col), lax.rem(c + 1, n_col)
-    peers = [{'row': lax.rem(r + i, n_row), 'col': lax.rem(c + j, n_col)} for i in range(n_row) for j in range(n_col) if i or j]
+    row_peers = [{'row': lax.rem(r + k, n_row)} for k in range(1, n_row)]
+    col_peers = [{'col': lax.rem(c + k, n_col)} for k in range(1, n_col)]
+    diag = [{'row': a, 'col': b} for a in (up, down) for b in (left, right)] if halo else []
+    peers = row_peers + col_peers + diag
     barrier = pltpu.get_barrier_semaphore()
     for peer in peers:
         pl.semaphore_signal(barrier, inc=1, device_id=peer, device_id_type=MESH)
@@ -105,8 +123,8 @@
     def copy(src, dst, slot, peer):
         return pltpu.make_async_remote_copy(src_ref=src, dst_ref=dst, send_sem=send.at[slot], recv_sem=recv.at[slot], device_id=peer, device_id_type=MESH)
 
-    copies = [copy(part_ref, buf.at[k], k, peer) for k, peer in enumerate(peers)]
-    for cp in copies:
+    first = [copy(part_ref, rbuf.at[k], k, peer) for k, peer in enumerate(row_peers)]
+    for cp in first:
         cp.start()
     halos = []
     if halo:
@@ -122,17 +140,24 @@
             (edge_ref.at[1, 0], side_ref.at[0, end], {'row': up, 'col': right}),
             (edge_ref.at[1, last], side_ref.at[0, 0], {'row': down, 'col': right}),
         ]
-        halos = [copy(src, dst, len(peers) + i, peer) for i, (src, dst, peer) in enumerate(plan)]
+        halos = [copy(src, dst, n_row + n_col - 2 + i, peer) for i, (src, dst, peer) in enumerate(plan)]
         for cp in halos:
             cp.start()
     total = part_ref[...]
-    for k, cp in enumerate(copies):
+    for k, cp in enumerate(first):
         cp.wait_recv()
-        total = total + buf[k]
+        total = total + rbuf[k]
+    rsum[...] = total
+    second = [copy(rsum, cbuf.at[k], n_row - 1 + k, peer) for k, peer in enumerate(col_peers)]
+    for cp in second:
+        cp.start()
+    for k, cp in enumerate(second):
+        cp.wait_recv()
+        total = total + cbuf[k]
     tot_ref[...] = total
     for cp in halos:
         cp.wait_recv()
-    for cp in copies + halos:
+    for cp in first + second + halos:
         cp.wait_send()
 
 
@@ -150,15 +175,16 @@
         ]
         args += [x, edge]
         in_specs += [ASPEC, VSPEC]
-    n_peer = n_row * n_col - 1
-    n_sem = n_peer + (8 if halo else 0)
+    n_sem = n_row + n_col - 2 + (8 if halo else 0)
     return pl.pallas_call(
         functools.partial(exchange_kernel, n_row, n_col, halo),
         out_shape=out_shape,
         in_specs=in_specs,
         out_specs=[VSPEC] + [ASPEC] * (len(out_shape) - 1),
         scratch_shapes=[
-            pltpu.VMEM((n_peer, 8, LANES), F32),
+            pltpu.VMEM((n_row - 1, 8, LANES), F32),
+            pltpu.VMEM((n_col - 1, 8, LANES), F32),
+            pltpu.VMEM((8, LANES), F32),
             pltpu.SemaphoreType.DMA((n_sem,)),
             pltpu.SemaphoreType.DMA((n_sem,)),
         ],
@@ -167,10 +193,11 @@
     )(*args)
 
 
-def conv_kernel(blk, idx, n_row, n_col, count, residual, x_ref, top_ref, bot_ref, side_ref, tot_ref, norm_ref, add_ref, w_hbm,
+def conv_kernel(idx, n_row, n_col, count, residual, blk_ref, x_ref, top_ref, bot_ref, side_ref, tot_ref, norm_ref, add_ref, w_hbm,
                 out_ref, edge_ref, part_ref, act, hside, stat, wbuf, acc, csum, sem):
     n_img, n_rows, n_cols, n_chan = x_ref.shape
     per_img = n_rows * n_cols
+    blk = blk_ref[0]
 
     def fetch(dy):
         return pltpu.make_async_copy(w_hbm.at[blk, idx, dy], wbuf.at[dy], sem.at[dy])
@@ -227,7 +254,7 @@
         acc[...] = add_ref[...].reshape(acc.shape).astype(F32)
     else:
         for b in range(n_img):
-            acc[b * per_img:(b + 1) * per_img, :] = jnp.broadcast_to(add_ref[b:b + 1, :], (per_img, n_chan))
+            acc[b * per_img:(b + 1) * per_img, :] = jnp.broadcast_to(add_ref[blk, b:b + 1, :], (per_img, n_chan))
 
     def taps(dy, carry):
         fetch(dy).wait()
@@ -247,9 +274,9 @@
     count = float(n_rows * n_cols * n_row * n_col * (n_chan // GROUPS))
     n_tok = n_img * n_rows * n_cols
     return pl.pallas_call(
-        functools.partial(conv_kernel, blk, idx, n_row, n_col, count, residual),
+        functools.partial(conv_kernel, idx, n_row, n_col, count, residual),
         out_shape=[jax.ShapeDtypeStruct(x.shape, BF16)] + finish_shapes(x.shape),
-        in_specs=[VSPEC] * 7 + [ASPEC],
+        in_specs=[pl.BlockSpec(memory_space=pltpu.SMEM)] + [VSPEC] * 7 + [ASPEC],
         out_specs=[VSPEC] * 3,
         scratch_shapes=[
             pltpu.VMEM((n_img, n_rows + 2, n_cols, 3 * n_chan), BF16),
@@ -263,19 +290,24 @@
         compiler_params=pltpu.CompilerParams(vmem_limit_bytes=VMEM_LIMIT),
         cost_estimate=pl.CostEstimate(flops=2 * 9 * n_tok * n_chan * n_chan, bytes_accessed=9 * 2 * n_chan * n_chan, transcendentals=n_tok * n_chan),
         name="conv",
-    )(x, top, bot, side, tot, norm, add, weights)
+    )(jnp.full((1,), blk, jnp.int32), x, top, bot, side, tot, norm, add, weights)
 
 
 def head_blocks(per_dev):
     return [(i, min(2, per_dev - i)) for i in range(0, per_dev, 2)]
+
+
+def send_plan(per_dev):
+    blocks = head_blocks(per_dev)
+    return [p for p in (blocks[:1], blocks[1:]) if p]
 
 
 def proj_kernel(count, per_dev, x_ref, tot_ref, norm_ref, w_ref, *refs):
     n_img, n_rows, n_cols, n_chan = x_ref.shape
     per_img = n_rows * n_cols
     hd = w_ref.shape[2]
-    blocks = head_blocks(per_dev)
-    outs, g, wcat = refs[:len(blocks)], refs[-2], refs[-1]
+    plan = send_plan(per_dev)
+    outs, g, wcat = refs[:len(plan)], refs[-2], refs[-1]
 
     @pl.when(pl.program_id(0) == 0)
     def _():
@@ -286,17 +318,20 @@
             z = x_ref[b].reshape(per_img, n_chan).astype(F32)
             g[b * per_img:(b + 1) * per_img, :] = ((z - st[b:b + 1]) * (st[2 + b:3 + b] * gain) + shift).astype(BF16)
 
-    for (first, n), out_ref in zip(blocks, outs):
-        for i in range(n):
-            wcat[2 * i * hd:(2 * i + 1) * hd, :] = w_ref[1, first + i]
-            wcat[(2 * i + 1) * hd:(2 * i + 2) * hd, :] = w_ref[2, first + i]
-            wcat[(2 * n + i) * hd:(2 * n + i + 1) * hd, :] = w_ref[0, first + i]
-        width = out_ref.shape[3]
-        if n == 1:
-            wcat[3 * hd:width, :] = jnp.zeros((width - 3 * hd, n_chan), BF16)
-        res = lax.dot_general(g[...], wcat[0:width, :], (((1,), (1,)), ((), ())), preferred_element_type=F32).astype(BF16)
-        for b in range(n_img):
-            out_ref[b, 0] = res[b * per_img:(b + 1) * per_img]
+    for blocks, out_ref in zip(plan, outs):
+        off = 0
+        for first, n in blocks:
+            for i in range(n):
+                wcat[2 * i * hd:(2 * i + 1) * hd, :] = w_ref[1, first + i]
+                wcat[(2 * i + 1) * hd:(2 * i + 2) * hd, :] = w_ref[2, first + i]
+                wcat[(2 * n + i) * hd:(2 * n + i + 1) * hd, :] = w_ref[0, first + i]
+            width = 2 * hd * (n + 1)
+            if n == 1:
+                wcat[3 * hd:width, :] = jnp.zeros((width - 3 * hd, n_chan), BF16)
+            res = lax.dot_general(g[...], wcat[0:width, :], (((1,), (1,)), ((), ())), preferred_element_type=F32).astype(BF16)
+            for b in range(n_img):
+                out_ref[b, 0, :, off:off + width] = res[b * per_img:(b + 1) * per_img]
+            off += width
 
 
 def proj(x, tot, norm, weights, n_row, n_col, per_dev):
@@ -305,7 +340,7 @@
     count = float(n_rows * n_cols * n_row * n_col * (n_chan // GROUPS))
     n_grp = n_heads // per_dev
     n_tok = n_rows * n_cols
-    widths = [2 * hd * (n + 1) for _, n in head_blocks(per_dev)]
+    widths = [sum(2 * hd * (n + 1) for _, n in blocks) for blocks in send_plan(per_dev)]
     return pl.pallas_call(
         functools.partial(proj_kernel, count, per_dev),
         grid=(n_grp,),
@@ -317,7 +352,7 @@
             pl.BlockSpec((3, per_dev, hd, n_chan), lambda q: (0, q, 0, 0)),
         ],
         out_specs=[pl.BlockSpec((n_img, 1, n_tok, w), lambda q: (0, q, 0, 0)) for w in widths],
-        scratch_shapes=[pltpu.VMEM((n_img * n_tok, n_chan), BF16), pltpu.VMEM((max(widths), n_chan), BF16)],
+        scratch_shapes=[pltpu.VMEM((n_img * n_tok, n_chan), BF16), pltpu.VMEM((6 * hd, n_chan), BF16)],
         compiler_params=pltpu.CompilerParams(vmem_limit_bytes=VMEM_LIMIT),
         cost_estimate=pl.CostEstimate(flops=2 * n_img * n_tok * n_chan * n_grp * sum(widths), bytes_accessed=6 * n_chan * n_chan, transcendentals=0),
         name="proj",
@@ -503,9 +538,7 @@
 def solution(mesh):
     n_row, n_col = mesh.shape['row'], mesh.shape['col']
 
-    def res_block(blk, x, edge, part, t_emb, res_norm, res_conv, res_temb):
-        t_act = jax.nn.silu(t_emb.astype(F32)).astype(BF16)
-        t_proj = jnp.dot(t_act, res_temb[blk], preferred_element_type=F32)
+    def res_block(blk, x, edge, part, t_proj, res_norm, res_conv):
         halos = exchange(part, n_row, n_col, x, edge)
         h, edge, part = conv(blk, 0, x, halos, res_norm, t_proj, res_conv, n_row, n_col, False)
         halos = exchange(part, n_row, n_col, h, edge)
@@ -519,23 +552,24 @@
         n_tok = n_rows * n_cols
         tot, = exchange(part, n_row, n_col)
         qkv = proj(x, tot, norm, weights, n_row, n_col, per_dev)
-        blocks = head_blocks(per_dev)
-        outs = [None] * len(blocks)
-        for k in sorted(range(len(blocks)), key=lambda k: blocks[k][1]):
-            n_pair = blocks[k][1]
-            kv_width = n_pair * 2 * hd
-            mine = lax.all_to_all(qkv[k].reshape(n_row, n_tok, -1), 'row', 0, 0).reshape(n_row * n_tok, -1)
-            kv = lax.all_gather(mine[:, :kv_width], 'col', axis=0, tiled=True)
-            out = attend(mine[:, kv_width:], kv, hd, n_pair)
-            out = lax.all_to_all(out.reshape(n_row, n_tok, 2 * hd), 'row', 0, 0)
-            outs[k] = out.reshape(n_img, -1, n_tok, 2 * hd)
+        outs = []
+        for sent, blocks in zip(qkv, send_plan(per_dev)):
+            mine = lax.all_to_all(sent.reshape(n_row, n_tok, -1), 'row', 0, 0).reshape(n_row * n_tok, -1)
+            off = 0
+            for _, n_pair in blocks:
+                mid, end = off + n_pair * 2 * hd, off + (n_pair + 1) * 2 * hd
+                kv = lax.all_gather(mine[:, off:mid], 'col', axis=0, tiled=True)
+                out = attend(mine[:, mid:end], kv, hd, n_pair)
+                out = lax.all_to_all(out.reshape(n_row, n_tok, 2 * hd), 'row', 0, 0)
+                outs.append(out.reshape(n_img, -1, n_tok, 2 * hd))
+                off = end
         return outproj(outs, weights, x, per_dev)
 
     def run_stage(latent, t_emb, res_norm, res_conv, res_temb, attn_norm, attn_proj):
-        edge, part = prep(latent)
-        x, edge, part = res_block(0, latent, edge, part, t_emb, res_norm, res_conv, res_temb)
+        edge, part, t_proj = prep(latent, t_emb, res_temb)
+        x, edge, part = res_block(0, latent, edge, part, t_proj, res_norm, res_conv)
         x, edge, part = attn_block(x, part, attn_norm, attn_proj)
-        return res_block(1, x, edge, part, t_emb, res_norm, res_conv, res_temb)[0]
+        return res_block(1, x, edge, part, t_proj, res_norm, res_conv)[0]
 
     spec_x = P('dp', 'row', 'col', None)
     return jax.shard_map(run_stage, mesh=mesh, in_specs=(spec_x, P('dp', None), P(), P(), P(), P(), P()), out_specs=spec_x, check_vma=False)

time: 339 us -> 345 us (1.018)
  waiting for transfers between devices: 10 us -> 25.7 us
  blocking collectives: 55.9 us -> 63.7 us
  matrix products: 6.17 us -> 0 us
  starting transfers between devices: 14.8 us -> 9.54 us
  Pallas kernels: 229 us -> 225 us
    all_gather x3, waiting for transfers between devices: 5.42 us -> 25.5 us  [attn_block(): kv = lax.all_gather(mine[:, off:mid], 'col', axis=0, tiled=True)]
    pallas_call x5, Pallas kernels: 66 us -> 57.4 us  [exchange(): pl.pallas_call(functools.partial(exchange_kernel, n_row, n_col, halo), ou...]
    all_to_all x3, blocking collectives: 55.9 us -> 63.7 us  [the longest x2 50.4 us: attn_block(): lax.all_to_all(sent.reshape(n_row, n_tok, -1), 'row', 0, 0)]
    dot_general x2 -> x0, matrix products: 6.17 us -> none  [res_block(): t_proj = jnp.dot(t_act, res_temb[blk], preferred_element_type=F32)]
    all_to_all x3 -> x2, starting transfers between devices: 14.7 us -> 9.41 us  [attn_block(): out = lax.all_to_all(out.reshape(n_row, n_tok, 2 * hd), 'row', 0, 0)]
    all_to_all x3 -> x2, waiting for transfers between devices: 4.46 us -> 0.01 us  [attn_block(): out = lax.all_to_all(out.reshape(n_row, n_tok, 2 * hd), 'row', 0, 0)]
    pallas_call x5, Pallas kernels: 78.9 us -> 83 us  [the longest x4 77.6 us: conv(): pl.pallas_call(functools.partial(conv_kernel, idx, n_row, n_col, count, r...]
  transfers between devices with their start and end apart: 6 -> 5, of which waited for: 2 -> 2; matrix products, arithmetic and copies ran while one was open for 2% -> 1% of each run, Pallas kernels for 20% -> 20%
where the time goes in v3:
time: 345 us; the launch traced here: 341 us
  Pallas kernels  225 us (65%)
  blocking collectives  63.7 us (18%)
  waiting for transfers between devices  25.7 us (7%)
  between operations  13.5 us (4%)
  starting transfers between devices  9.54 us (3%)
  local copies, waits for them, and re-layouts  3.76 us (1%)
    pallas_call x4, Pallas kernels, conv(): pl.pallas_call(functools.partial(conv_kernel, idx, n_row, n_col, count, r...  77.6 us
    pallas_call x3, Pallas kernels, attend(): pl.pallas_call(functools.partial(attend_kernel, hd, n_pair), grid=(n_pair...  66.9 us
    pallas_call x5, Pallas kernels, exchange(): pl.pallas_call(functools.partial(exchange_kernel, n_row, n_col, halo), ou...  57.4 us
    all_to_all x2, blocking collectives, attn_block(): lax.all_to_all(sent.reshape(n_row, n_tok, -1), 'row', 0, 0)  50.4 us
    all_gather x3, waiting for transfers between devices, attn_block(): kv = lax.all_gather(mine[:, off:mid], 'col', axis=0, tiled=True)  25.5 us
    all_to_all x1, blocking collectives, attn_block(): out = lax.all_to_all(out.reshape(n_row, n_tok, 2 * hd), 'row', 0, 0)  13.3 us
    pallas_call x1, Pallas kernels, proj(): pl.pallas_call(functools.partial(proj_kernel, count, per_dev), grid=(n_gr...  10.1 us
    all_to_all x2, starting transfers between devices, attn_block(): out = lax.all_to_all(out.reshape(n_row, n_tok, 2 * hd), 'row', 0, 0)  9.41 us
  transfers between devices with their start and end apart: 5, of which 2 were waited for; matrix products, arithmetic and copies ran while one was open for 1% of the time, Pallas kernels for 20%

profile of v3, /device:TPU:97, one launch (start us, length us, event | category | flops | bytes accessed | tf_op | source)
XLA Modules:
  0.0 340.8 jit_solution(16116530475914885686)
XLA Ops:
  6.5 0.0 all-gather.8.cloned.1.call-start
  6.6 5.4 %prep.1 = (bf16[2,4,2,1280]{3,2,1,0:T(2,128)(2,1)}, f32[8,128]{1,0:T(8,128)}, f32[2,2,1280]{2,1,0:T(2,128)}) custom-call(bf16[2,4,48,1280]{3,2,1,0:T(8,128)(2,1)} %add_ref.1, bf16[2,1280]{1,0:T(2,128)(2,1)} %emb_ref.1, bf16[2,1280,1280]{2,1,0:T(8,128)(2,1)} %w_hbm.5), custom_call_target="tpu_custom_call" | custom-call | tf_op jit(solution)/shard_map/prep/pallas_call | solution.py:89
  12.0 15.3 %exchange.5 = (f32[8,128]{1,0:T(8,128)}, bf16[2,48,1280]{2,1,0:T(8,128)(2,1)}, bf16[2,48,1280]{2,1,0:T(8,128)(2,1)}, bf16[2,6,2,1280]{3,2,1,0:T(2,128)(2,1)}) custom-call(f32[8,128]{1,0:T(8,128)} %get-tuple-element.38.refs_0_, bf16[2,4,48,1280]{3,2,1,0:T(8,128)(2,1)} %add_ref.1, bf16[2,4,2,1280]{3,2,1,0:T(2,128)(2,1)} %get-tuple-element.39.refs_2_), custom_call_target="tpu_custom_call" | custom-call | tf_op jit(solution)/shard_map/exchange/pallas_call | solution.py:179
  27.3 19.2 %conv.4 = (bf16[2,4,48,1280]{3,2,1,0:T(8,128)(2,1)}, bf16[2,4,2,1280]{3,2,1,0:T(2,128)(2,1)}, f32[8,128]{1,0:T(8,128)}) custom-call(s32[1]{0:T(128)} %constant.1.clone.1.blk_ref, bf16[2,4,48,1280]{3,2,1,0:T(8,128)(2,1)} %add_ref.1, bf16[2,48,1280]{2,1,0:T(8,128)(2,1)} %get-tuple-element.40.top_ref, bf16[2,48,1280]{2,1,0:T(8,128)(2,1)} %get-tuple-element.41.bot_ref, ...), custom_call_target="tpu_custom_call" | custom-call | flops 11324620800 | bytes 29491200 | tf_op jit(solution)/shard_map/conv/pallas_call | solution.py:276
  46.5 10.9 %exchange.6 = (f32[8,128]{1,0:T(8,128)}, bf16[2,48,1280]{2,1,0:T(8,128)(2,1)}, bf16[2,48,1280]{2,1,0:T(8,128)(2,1)}, bf16[2,6,2,1280]{3,2,1,0:T(2,128)(2,1)}) custom-call(f32[8,128]{1,0:T(8,128)} %get-tuple-element.46.refs_0_, bf16[2,4,48,1280]{3,2,1,0:T(8,128)(2,1)} %get-tuple-element.45.refs_1_.x_ref, bf16[2,4,2,1280]{3,2,1,0:T(2,128)(2,1)} %get-tuple-element.47.refs_2_), custom_call_target="tpu_custom_call" | custom-call | tf_op jit(solution)/shard_map/exchange/pallas_call | solution.py:179
  57.5 19.6 %conv.5 = (bf16[2,4,48,1280]{3,2,1,0:T(8,128)(2,1)}, bf16[2,4,2,1280]{3,2,1,0:T(2,128)(2,1)}, f32[8,128]{1,0:T(8,128)}) custom-call(s32[1]{0:T(128)} %constant.1.clone.1.blk_ref, bf16[2,4,48,1280]{3,2,1,0:T(8,128)(2,1)} %get-tuple-element.45.refs_1_.x_ref, bf16[2,48,1280]{2,1,0:T(8,128)(2,1)} %get-tuple-element.48.top_ref, ...), custom_call_target="tpu_custom_call" | custom-call | flops 11324620800 | bytes 29491200 | tf_op jit(solution)/shard_map/conv/pallas_call | solution.py:276
  77.1 10.0 %exchange.7.tot_ref = f32[8,128]{1,0:T(8,128)} custom-call(f32[8,128]{1,0:T(8,128)} %get-tuple-element.53.refs_0_), custom_call_target="tpu_custom_call" | custom-call | tf_op jit(solution)/shard_map/exchange/pallas_call | solution.py:179
  87.1 10.1 %proj.1 = (bf16[2,4,192,384]{3,2,1,0:T(8,128)(2,1)}, bf16[2,4,192,640]{3,2,1,0:T(8,128)(2,1)}) custom-call(bf16[2,4,48,1280]{3,2,1,0:T(8,128)(2,1)} %get-tuple-element.52.x_ref.refs_4_, f32[8,128]{1,0:T(8,128)} %exchange.7.tot_ref, bf16[2,1280]{1,0:T(2,128)(2,1)} %norm_ref.7, bf16[4,20,64,1280]{3,2,1,0:T(8,128)(2,1)} %bitcast.11), custom_call_target="tpu_custom_call" | custom-call | flops 4026531840 | bytes 9830400 | tf_op jit(solution)/shard_map/proj/pallas_call | solution.py:344
  97.2 29.5 %all_to_all.25 = bf16[8,192,640]{2,1,0:T(8,128)(2,1)S(1)} all-to-all(bf16[8,192,640]{2,1,0:T(8,128)(2,1)} %bitcast.17), channel_id=1, replica_groups=mesh['dp'=1,'col'=4,'row'=8] {'row'}, dimensions={0} | all-to-all | bytes 3932160 | tf_op jit(solution)/shard_map/all_to_all | solution.py:557
  126.7 1.1 fusion
  127.8 0.1 all-gather.8.cloned.1.call-update
  127.9 0.1 all-gather.4.cloned.1.call-start
  128.0 20.9 %all_to_all.26 = bf16[8,192,384]{2,1,0:T(8,128)(2,1)S(1)} all-to-all(bf16[8,192,384]{2,1,0:T(8,128)(2,1)} %bitcast.21), channel_id=1, replica_groups=mesh['dp'=1,'col'=4,'row'=8] {'row'}, dimensions={0} | all-to-all | bytes 2359296 | tf_op jit(solution)/shard_map/all_to_all | solution.py:557
  148.9 0.9 slice.25
  149.8 0.1 all-gather.4.cloned.1.call-update
  149.9 0.1 all-gather.6.cloned.1.call-start
  149.9 0.9 slice.27
  150.9 0.1 all-gather.6.cloned.1.call-update
  150.9 0.8 slice.24.q_ref
  151.7 0.0 all-gather.8.cloned.1.call-done.kv_ref
  151.7 14.3 %attend.5 = bf16[1536,128]{1,0:T(8,128)(2,1)} custom-call(bf16[1536,128]{1,0:T(8,128)(2,1)} %get-tuple-element.72.q_ref, bf16[6144,128]{1,0:T(8,128)(2,1)} %all-gather.8.cloned.1.call-done.kv_ref), custom_call_target="tpu_custom_call" | custom-call | flops 9663676416 | bytes 1572864 | tf_op jit(solution)/shard_map/attend/pallas_call | solution.py:470
  166.0 4.2 %all-to-all-start.4 = ((bf16[8,192,128]{2,1,0:T(8,128)(2,1)}), bf16[8,192,128]{2,1,0:T(8,128)(2,1)S(1)}, u32[]{:S(2)}, u32[]{:S(2)}) async-start(bf16[8,192,128]{2,1,0:T(8,128)(2,1)} %bitcast.23), calls=%async_computation.4 | async-start | bytes 786432 | tf_op jit(solution)/shard_map/all_to_all | solution.py:563
  170.2 18.4 %all-gather.4.cloned.1.call-done.kv_ref = bf16[6144,256]{1,0:T(8,128)(2,1)} async-done(((bf16[1536,256]{1,0:T(8,128)(2,1)}), bf16[6144,256]{1,0:T(8,128)(2,1)}) %all-gather.4.cloned.1.call-update) | async-done | bytes 3145744 | tf_op jit(solution)/shard_map/all_gather | solution.py:561
  188.6 26.3 %attend.3 = bf16[1536,128]{1,0:T(8,128)(2,1)} custom-call(bf16[1536,128]{1,0:T(8,128)(2,1)} %slice.24.q_ref, bf16[6144,256]{1,0:T(8,128)(2,1)} %all-gather.4.cloned.1.call-done.kv_ref), custom_call_target="tpu_custom_call" | custom-call | flops 19327352832 | bytes 3145728 | tf_op jit(solution)/shard_map/attend/pallas_call | solution.py:470
  214.9 0.0 all-to-all-done.4
  214.9 0.0 copy-start
  214.9 5.2 %all-to-all-start.1 = ((bf16[8,192,128]{2,1,0:T(8,128)(2,1)}), bf16[8,192,128]{2,1,0:T(8,128)(2,1)S(1)}, u32[]{:S(2)}, u32[]{:S(2)}) async-start(bf16[8,192,128]{2,1,0:T(8,128)(2,1)} %bitcast.22), calls=%async_computation.1 | async-start | bytes 786432 | tf_op jit(solution)/shard_map/all_to_all | solution.py:563
  220.1 7.1 %all-gather.6.cloned.1.call-done.kv_ref = bf16[6144,256]{1,0:T(8,128)(2,1)} async-done(((bf16[1536,256]{1,0:T(8,128)(2,1)}), bf16[6144,256]{1,0:T(8,128)(2,1)}) %all-gather.6.cloned.1.call-update) | async-done | bytes 3145744 | tf_op jit(solution)/shard_map/all_gather | solution.py:561
  227.2 26.3 %attend.4 = bf16[1536,128]{1,0:T(8,128)(2,1)} custom-call(bf16[1536,128]{1,0:T(8,128)(2,1)} %get-tuple-element.73.q_ref, bf16[6144,256]{1,0:T(8,128)(2,1)} %all-gather.6.cloned.1.call-done.kv_ref), custom_call_target="tpu_custom_call" | custom-call | flops 19327352832 | bytes 3145728 | tf_op jit(solution)/shard_map/attend/pallas_call | solution.py:470
  253.5 0.0 copy-done
  253.5 0.0 all-to-all-done.1
  253.5 0.0 copy-start.1
  253.5 13.3 %all_to_all.27 = bf16[8,192,128]{2,1,0:T(8,128)(2,1)} all-to-all(bf16[8,192,128]{2,1,0:T(8,128)(2,1)} %bitcast.24), channel_id=1, replica_groups=mesh['dp'=1,'col'=4,'row'=8] {'row'}, dimensions={0} | all-to-all | bytes 786432 | tf_op jit(solution)/shard_map/all_to_all | solution.py:563
  266.8 0.0 copy-done.1
  266.8 7.2 %outproj.1 = (bf16[2,4,48,1280]{3,2,1,0:T(8,128)(2,1)}, bf16[2,4,2,1280]{3,2,1,0:T(2,128)(2,1)}, f32[8,128]{1,0:T(8,128)}) custom-call(bf16[2,4,192,128]{3,2,1,0:T(8,128)(2,1)} %bitcast.19, bf16[2,4,192,128]{3,2,1,0:T(8,128)(2,1)} %bitcast.20, bf16[2,4,192,128]{3,2,1,0:T(8,128)(2,1)} %bitcast.18, bf16[4,20,64,1280]{3,2,1,0:T(8,128)(2,1)} %bitcast.12, ...), custom_call_target="tpu_custom_call" | custom-call | flops 1258291200 | bytes 3276800 | tf_op jit(solution)/shard_map/outproj/pallas_call | solution.py:522
  274.0 10.4 %exchange.8 = (f32[8,128]{1,0:T(8,128)}, bf16[2,48,1280]{2,1,0:T(8,128)(2,1)}, bf16[2,48,1280]{2,1,0:T(8,128)(2,1)}, bf16[2,6,2,1280]{3,2,1,0:T(2,128)(2,1)}) custom-call(f32[8,128]{1,0:T(8,128)} %get-tuple-element.57.refs_0_, bf16[2,4,48,1280]{3,2,1,0:T(8,128)(2,1)} %get-tuple-element.56.refs_1_.x_ref.add_ref, bf16[2,4,2,1280]{3,2,1,0:T(2,128)(2,1)} %get-tuple-element.58.refs_2_), custom_call_target="tpu_custom_call" | custom-call | tf_op jit(solution)/shard_map/exchange/pallas_call | solution.py:179
  284.4 19.2 %conv.6 = (bf16[2,4,48,1280]{3,2,1,0:T(8,128)(2,1)}, bf16[2,4,2,1280]{3,2,1,0:T(2,128)(2,1)}, f32[8,128]{1,0:T(8,128)}) custom-call(s32[1]{0:T(128)} %constant.0.clone.1.blk_ref, bf16[2,4,48,1280]{3,2,1,0:T(8,128)(2,1)} %get-tuple-element.56.refs_1_.x_ref.add_ref, bf16[2,48,1280]{2,1,0:T(8,128)(2,1)} %get-tuple-element.59.top_ref, ...), custom_call_target="tpu_custom_call" | custom-call | flops 11324620800 | bytes 29491200 | tf_op jit(solution)/shard_map/conv/pallas_call | solution.py:276
  303.6 10.7 %exchange.9 = (f32[8,128]{1,0:T(8,128)}, bf16[2,48,1280]{2,1,0:T(8,128)(2,1)}, bf16[2,48,1280]{2,1,0:T(8,128)(2,1)}, bf16[2,6,2,1280]{3,2,1,0:T(2,128)(2,1)}) custom-call(f32[8,128]{1,0:T(8,128)} %get-tuple-element.64.refs_0_, bf16[2,4,48,1280]{3,2,1,0:T(8,128)(2,1)} %get-tuple-element.63.refs_1_.x_ref, bf16[2,4,2,1280]{3,2,1,0:T(2,128)(2,1)} %get-tuple-element.65.refs_2_), custom_call_target="tpu_custom_call" | custom-call | tf_op jit(solution)/shard_map/exchange/pallas_call | solution.py:179
  314.4 19.5 %conv.7 = (bf16[2,4,48,1280]{3,2,1,0:T(8,128)(2,1)}, bf16[2,4,2,1280]{3,2,1,0:T(2,128)(2,1)}, f32[8,128]{1,0:T(8,128)}) custom-call(s32[1]{0:T(128)} %constant.0.clone.1.blk_ref, bf16[2,4,48,1280]{3,2,1,0:T(8,128)(2,1)} %get-tuple-element.63.refs_1_.x_ref, bf16[2,48,1280]{2,1,0:T(8,128)(2,1)} %get-tuple-element.66.top_ref, ...), custom_call_target="tpu_custom_call" | custom-call | flops 11324620800 | bytes 29491200 | tf_op jit(solution)/shard_map/conv/pallas_call | solution.py:276
Async XLA Ops:
  6.5 145.1 %all-gather.8.cloned.1.call-start = ((), (), s32[]{:S(2)}) async-start(), calls=%async_computation.7 | async-start | bytes 1966080 | tf_op jit(solution)/shard_map/all_gather | solution.py:561
  127.9 60.7 %all-gather.4.cloned.1.call-start = ((), (), s32[]{:S(2)}) async-start(), calls=%async_computation.5 | async-start | bytes 3932160 | tf_op jit(solution)/shard_map/all_gather | solution.py:561
  149.9 77.3 %all-gather.6.cloned.1.call-start = ((), (), s32[]{:S(2)}) async-start(), calls=%async_computation.6 | async-start | bytes 3932160 | tf_op jit(solution)/shard_map/all_gather | solution.py:561
  166.0 48.9 %all-to-all-start.4 = ((bf16[8,192,128]{2,1,0:T(8,128)(2,1)}), bf16[8,192,128]{2,1,0:T(8,128)(2,1)S(1)}, u32[]{:S(2)}, u32[]{:S(2)}) async-start(bf16[8,192,128]{2,1,0:T(8,128)(2,1)} %bitcast.23), calls=%async_computation.4 | async-start | bytes 786432 | tf_op jit(solution)/shard_map/all_to_all | solution.py:563
  214.9 38.6 %copy-start = (bf16[8,192,128]{2,1,0:T(8,128)(2,1)}, bf16[8,192,128]{2,1,0:T(8,128)(2,1)S(1)}, u32[]{:S(2)}) copy-start(bf16[8,192,128]{2,1,0:T(8,128)(2,1)S(1)} %all-to-all-done.4) | copy-start | bytes 1179652
  214.9 38.6 %all-to-all-start.1 = ((bf16[8,192,128]{2,1,0:T(8,128)(2,1)}), bf16[8,192,128]{2,1,0:T(8,128)(2,1)S(1)}, u32[]{:S(2)}, u32[]{:S(2)}) async-start(bf16[8,192,128]{2,1,0:T(8,128)(2,1)} %bitcast.22), calls=%async_computation.1 | async-start | bytes 786432 | tf_op jit(solution)/shard_map/all_to_all | solution.py:563
  253.5 13.3 %copy-start.1 = (bf16[8,192,128]{2,1,0:T(8,128)(2,1)}, bf16[8,192,128]{2,1,0:T(8,128)(2,1)S(1)}, u32[]{:S(2)}) copy-start(bf16[8,192,128]{2,1,0:T(8,128)(2,1)S(1)} %all-to-all-done.1) | copy-start | bytes 1179652
Sparse Core Ops, SparseCore 0:
  128.0 22.1 all-gather.7
  151.8 36.8 all-gather.3
  190.2 36.9 all-gather.5

commit v4 on v3

--- a/solution.py
+++ b/solution.py
@@ -193,11 +193,10 @@
     )(*args)
 
 
-def conv_kernel(idx, n_row, n_col, count, residual, blk_ref, x_ref, top_ref, bot_ref, side_ref, tot_ref, norm_ref, add_ref, w_hbm,
+def conv_kernel(blk, idx, n_row, n_col, count, residual, x_ref, top_ref, bot_ref, side_ref, tot_ref, norm_ref, add_ref, w_hbm,
                 out_ref, edge_ref, part_ref, act, hside, stat, wbuf, acc, csum, sem):
     n_img, n_rows, n_cols, n_chan = x_ref.shape
     per_img = n_rows * n_cols
-    blk = blk_ref[0]
 
     def fetch(dy):
         return pltpu.make_async_copy(w_hbm.at[blk, idx, dy], wbuf.at[dy], sem.at[dy])
@@ -274,9 +273,9 @@
     count = float(n_rows * n_cols * n_row * n_col * (n_chan // GROUPS))
     n_tok = n_img * n_rows * n_cols
     return pl.pallas_call(
-        functools.partial(conv_kernel, idx, n_row, n_col, count, residual),
+        functools.partial(conv_kernel, blk, idx, n_row, n_col, count, residual),
         out_shape=[jax.ShapeDtypeStruct(x.shape, BF16)] + finish_shapes(x.shape),
-        in_specs=[pl.BlockSpec(memory_space=pltpu.SMEM)] + [VSPEC] * 7 + [ASPEC],
+        in_specs=[VSPEC] * 7 + [ASPEC],
         out_specs=[VSPEC] * 3,
         scratch_shapes=[
             pltpu.VMEM((n_img, n_rows + 2, n_cols, 3 * n_chan), BF16),
@@ -290,7 +289,7 @@
         compiler_params=pltpu.CompilerParams(vmem_limit_bytes=VMEM_LIMIT),
         cost_estimate=pl.CostEstimate(flops=2 * 9 * n_tok * n_chan * n_chan, bytes_accessed=9 * 2 * n_chan * n_chan, transcendentals=n_tok * n_chan),
         name="conv",
-    )(jnp.full((1,), blk, jnp.int32), x, top, bot, side, tot, norm, add, weights)
+    )(x, top, bot, side, tot, norm, add, weights)
 
 
 def head_blocks(per_dev):
@@ -552,17 +551,28 @@
         n_tok = n_rows * n_cols
         tot, = exchange(part, n_row, n_col)
         qkv = proj(x, tot, norm, weights, n_row, n_col, per_dev)
-        outs = []
+        parts = []
+        mine = None
         for sent, blocks in zip(qkv, send_plan(per_dev)):
+            if mine is not None:
+                sent, mine = lax.optimization_barrier((sent, mine))
             mine = lax.all_to_all(sent.reshape(n_row, n_tok, -1), 'row', 0, 0).reshape(n_row * n_tok, -1)
             off = 0
             for _, n_pair in blocks:
                 mid, end = off + n_pair * 2 * hd, off + (n_pair + 1) * 2 * hd
-                kv = lax.all_gather(mine[:, off:mid], 'col', axis=0, tiled=True)
-                out = attend(mine[:, mid:end], kv, hd, n_pair)
-                out = lax.all_to_all(out.reshape(n_row, n_tok, 2 * hd), 'row', 0, 0)
-                outs.append(out.reshape(n_img, -1, n_tok, 2 * hd))
+                parts.append([mine[:, mid:end], mine[:, off:mid], n_pair])
                 off = end
+        outs = []
+        out = None
+        for k, (q, kv, n_pair) in enumerate(parts):
+            full = lax.all_gather(kv, 'col', axis=0, tiled=True)
+            if k + 1 < len(parts):
+                if out is not None:
+                    parts[k + 1][1], out = lax.optimization_barrier((parts[k + 1][1], out))
+                q, parts[k + 1][1] = lax.optimization_barrier((q, parts[k + 1][1]))
+            out = attend(q, full, hd, n_pair)
+            back = lax.all_to_all(out.reshape(n_row, n_tok, 2 * hd), 'row', 0, 0)
+            outs.append(back.reshape(n_img, -1, n_tok, 2 * hd))
         return outproj(outs, weights, x, per_dev)
 
     def run_stage(latent, t_emb, res_norm, res_conv, res_temb, attn_norm, attn_proj):

time: 345 us -> 328 us (0.951)
  blocking collectives: 63.7 us -> 33.9 us
  waiting for transfers between devices: 25.7 us -> 34.8 us
  starting transfers between devices: 9.54 us -> 15 us
    all_to_all x2 -> x1, blocking collectives: 50.4 us -> 21.1 us  [attn_block(): lax.all_to_all(sent.reshape(n_row, n_tok, -1), 'row', 0, 0)]
    all_to_all x2 -> x3, waiting for transfers between devices: 0.01 us -> 23.9 us  [the longest x1 23.9 us: attn_block(): lax.all_to_all(sent.reshape(n_row, n_tok, -1), 'row', 0, 0)]
    all_gather x3, waiting for transfers between devices: 25.5 us -> 10.8 us  [attn_block(): full = lax.all_gather(kv, 'col', axis=0, tiled=True)]
    all_to_all x2 -> x3, starting transfers between devices: 9.41 us -> 14.8 us  [the longest x2 10.4 us: attn_block(): back = lax.all_to_all(out.reshape(n_row, n_tok, 2 * hd), 'row', 0, 0)]
  transfers between devices with their start and end apart: 5 -> 6, of which waited for: 2 -> 3; matrix products, arithmetic and copies ran while one was open for 1% -> 1% of each run, Pallas kernels for 20% -> 21%
where the time goes in v4:
time: 328 us; the launch traced here: 324 us
  Pallas kernels  223 us (68%)
  waiting for transfers between devices  34.8 us (11%)
  blocking collectives  33.9 us (10%)
  starting transfers between devices  15 us (5%)
  between operations  13.5 us (4%)
  local copies, waits for them, and re-layouts  3.81 us (1%)
    pallas_call x4, Pallas kernels, conv(): pl.pallas_call(functools.partial(conv_kernel, blk, idx, n_row, n_col, cou...  76.1 us
    pallas_call x3, Pallas kernels, attend(): pl.pallas_call(functools.partial(attend_kernel, hd, n_pair), grid=(n_pair...  66.9 us
    pallas_call x5, Pallas kernels, exchange(): pl.pallas_call(functools.partial(exchange_kernel, n_row, n_col, halo), ou...  57.4 us
    all_to_all x1, waiting for transfers between devices, attn_block(): lax.all_to_all(sent.reshape(n_row, n_tok, -1), 'row', 0, 0)  23.9 us
    all_to_all x1, blocking collectives, attn_block(): lax.all_to_all(sent.reshape(n_row, n_tok, -1), 'row', 0, 0)  21.1 us
    all_to_all x1, blocking collectives, attn_block(): back = lax.all_to_all(out.reshape(n_row, n_tok, 2 * hd), 'row', 0, 0)  12.9 us
    all_gather x3, waiting for transfers between devices, attn_block(): full = lax.all_gather(kv, 'col', axis=0, tiled=True)  10.8 us
    all_to_all x2, starting transfers between devices, attn_block(): back = lax.all_to_all(out.reshape(n_row, n_tok, 2 * hd), 'row', 0, 0)  10.4 us
  transfers between devices with their start and end apart: 6, of which 3 were waited for; matrix products, arithmetic and copies ran while one was open for 1% of the time, Pallas kernels for 21%

profile of v4, /device:TPU:97, one launch (start us, length us, event | category | flops | bytes accessed | tf_op | source)
XLA Modules:
  0.0 324.2 jit_solution(18312920630563210068)
XLA Ops:
  6.5 0.0 all-gather.4.cloned.1.call-start
  6.6 5.4 %prep.1 = (bf16[2,4,2,1280]{3,2,1,0:T(2,128)(2,1)}, f32[8,128]{1,0:T(8,128)}, f32[2,2,1280]{2,1,0:T(2,128)}) custom-call(bf16[2,4,48,1280]{3,2,1,0:T(8,128)(2,1)} %add_ref.1, bf16[2,1280]{1,0:T(2,128)(2,1)} %emb_ref.1, bf16[2,1280,1280]{2,1,0:T(8,128)(2,1)} %w_hbm.5), custom_call_target="tpu_custom_call" | custom-call | tf_op jit(solution)/shard_map/prep/pallas_call | solution.py:89
  11.9 15.3 %exchange.5 = (f32[8,128]{1,0:T(8,128)}, bf16[2,48,1280]{2,1,0:T(8,128)(2,1)}, bf16[2,48,1280]{2,1,0:T(8,128)(2,1)}, bf16[2,6,2,1280]{3,2,1,0:T(2,128)(2,1)}) custom-call(f32[8,128]{1,0:T(8,128)} %get-tuple-element.44.refs_0_, bf16[2,4,48,1280]{3,2,1,0:T(8,128)(2,1)} %add_ref.1, bf16[2,4,2,1280]{3,2,1,0:T(2,128)(2,1)} %get-tuple-element.45.refs_2_), custom_call_target="tpu_custom_call" | custom-call | tf_op jit(solution)/shard_map/exchange/pallas_call | solution.py:179
  27.3 18.8 %conv.4 = (bf16[2,4,48,1280]{3,2,1,0:T(8,128)(2,1)}, bf16[2,4,2,1280]{3,2,1,0:T(2,128)(2,1)}, f32[8,128]{1,0:T(8,128)}) custom-call(bf16[2,4,48,1280]{3,2,1,0:T(8,128)(2,1)} %add_ref.1, bf16[2,48,1280]{2,1,0:T(8,128)(2,1)} %get-tuple-element.46.top_ref, bf16[2,48,1280]{2,1,0:T(8,128)(2,1)} %get-tuple-element.47.bot_ref, ...), custom_call_target="tpu_custom_call" | custom-call | flops 11324620800 | bytes 29491200 | tf_op jit(solution)/shard_map/conv/pallas_call | solution.py:275
  46.1 11.0 %exchange.6 = (f32[8,128]{1,0:T(8,128)}, bf16[2,48,1280]{2,1,0:T(8,128)(2,1)}, bf16[2,48,1280]{2,1,0:T(8,128)(2,1)}, bf16[2,6,2,1280]{3,2,1,0:T(2,128)(2,1)}) custom-call(f32[8,128]{1,0:T(8,128)} %get-tuple-element.52.refs_0_, bf16[2,4,48,1280]{3,2,1,0:T(8,128)(2,1)} %get-tuple-element.51.refs_1_.x_ref, bf16[2,4,2,1280]{3,2,1,0:T(2,128)(2,1)} %get-tuple-element.53.refs_2_), custom_call_target="tpu_custom_call" | custom-call | tf_op jit(solution)/shard_map/exchange/pallas_call | solution.py:179
  57.1 19.2 %conv.5 = (bf16[2,4,48,1280]{3,2,1,0:T(8,128)(2,1)}, bf16[2,4,2,1280]{3,2,1,0:T(2,128)(2,1)}, f32[8,128]{1,0:T(8,128)}) custom-call(bf16[2,4,48,1280]{3,2,1,0:T(8,128)(2,1)} %get-tuple-element.51.refs_1_.x_ref, bf16[2,48,1280]{2,1,0:T(8,128)(2,1)} %get-tuple-element.54.top_ref, bf16[2,48,1280]{2,1,0:T(8,128)(2,1)} %get-tuple-element.55.bot_ref, ...), custom_call_target="tpu_custom_call" | custom-call | flops 11324620800 | bytes 29491200 | tf_op jit(solution)/shard_map/conv/pallas_call | solution.py:275
  76.3 10.0 %exchange.7.tot_ref = f32[8,128]{1,0:T(8,128)} custom-call(f32[8,128]{1,0:T(8,128)} %get-tuple-element.59.refs_0_), custom_call_target="tpu_custom_call" | custom-call | tf_op jit(solution)/shard_map/exchange/pallas_call | solution.py:179
  86.3 10.1 %proj.1 = (bf16[2,4,192,384]{3,2,1,0:T(8,128)(2,1)}, bf16[2,4,192,640]{3,2,1,0:T(8,128)(2,1)}) custom-call(bf16[2,4,48,1280]{3,2,1,0:T(8,128)(2,1)} %get-tuple-element.58.x_ref.refs_4_, f32[8,128]{1,0:T(8,128)} %exchange.7.tot_ref, bf16[2,1280]{1,0:T(2,128)(2,1)} %norm_ref.7, bf16[4,20,64,1280]{3,2,1,0:T(8,128)(2,1)} %bitcast.11), custom_call_target="tpu_custom_call" | custom-call | flops 4026531840 | bytes 9830400 | tf_op jit(solution)/shard_map/proj/pallas_call | solution.py:343
  96.4 21.1 %all_to_all.25 = bf16[8,192,384]{2,1,0:T(8,128)(2,1)S(1)} all-to-all(bf16[8,192,384]{2,1,0:T(8,128)(2,1)} %bitcast.21), channel_id=1, replica_groups=mesh['dp'=1,'col'=4,'row'=8] {'row'}, dimensions={0} | all-to-all | bytes 2359296 | tf_op jit(solution)/shard_map/all_to_all | solution.py:559
  117.4 0.9 slice.26
  118.4 0.1 all-gather.4.cloned.1.call-update
  118.4 4.4 %all-to-all-start.1 = ((bf16[8,192,640]{2,1,0:T(8,128)(2,1)}), bf16[8,192,640]{2,1,0:T(8,128)(2,1)S(1)}, u32[]{:S(2)}, u32[]{:S(2)}) async-start(bf16[8,192,640]{2,1,0:T(8,128)(2,1)} %bitcast.17), calls=%async_computation.1 | async-start | bytes 3932160 | tf_op jit(solution)/shard_map/all_to_all | solution.py:559
  122.8 0.0 all-gather.6.cloned.1.call-start
  122.8 0.8 slice.24.q_ref
  123.6 23.9 %all-to-all-done.1 = bf16[8,192,640]{2,1,0:T(8,128)(2,1)S(1)} async-done(((bf16[8,192,640]{2,1,0:T(8,128)(2,1)}), bf16[8,192,640]{2,1,0:T(8,128)(2,1)S(1)}, u32[]{:S(2)}, u32[]{:S(2)}) %all-to-all-start.1) | async-done | bytes 1966112 | tf_op jit(solution)/shard_map/all_to_all | solution.py:559
  147.5 1.0 slice.25
  148.5 0.1 all-gather.6.cloned.1.call-update
  148.6 0.2 all-gather.8.cloned.1.call-start
  148.8 1.1 fusion
  149.9 3.8 %all-gather.4.cloned.1.call-done.kv_ref = bf16[6144,256]{1,0:T(8,128)(2,1)} async-done(((bf16[1536,256]{1,0:T(8,128)(2,1)}), bf16[6144,256]{1,0:T(8,128)(2,1)}) %all-gather.4.cloned.1.call-update) | async-done | bytes 3145744 | tf_op jit(solution)/shard_map/all_gather | solution.py:568
  153.7 26.3 %attend.3 = bf16[1536,128]{1,0:T(8,128)(2,1)} custom-call(bf16[1536,128]{1,0:T(8,128)(2,1)} %slice.24.q_ref, bf16[6144,256]{1,0:T(8,128)(2,1)} %all-gather.4.cloned.1.call-done.kv_ref), custom_call_target="tpu_custom_call" | custom-call | flops 19327352832 | bytes 3145728 | tf_op jit(solution)/shard_map/attend/pallas_call | solution.py:469
  180.0 0.1 all-gather.8.cloned.1.call-update
  180.0 5.2 %all-to-all-start.2 = ((bf16[8,192,128]{2,1,0:T(8,128)(2,1)}), bf16[8,192,128]{2,1,0:T(8,128)(2,1)S(1)}, u32[]{:S(2)}, u32[]{:S(2)}) async-start(bf16[8,192,128]{2,1,0:T(8,128)(2,1)} %bitcast.22), calls=%async_computation.2 | async-start | bytes 786432 | tf_op jit(solution)/shard_map/all_to_all | solution.py:574
  185.3 7.0 %all-gather.6.cloned.1.call-done.kv_ref = bf16[6144,256]{1,0:T(8,128)(2,1)} async-done(((bf16[1536,256]{1,0:T(8,128)(2,1)}), bf16[6144,256]{1,0:T(8,128)(2,1)}) %all-gather.6.cloned.1.call-update) | async-done | bytes 3145744 | tf_op jit(solution)/shard_map/all_gather | solution.py:568
  192.3 26.3 %attend.4 = bf16[1536,128]{1,0:T(8,128)(2,1)} custom-call(bf16[1536,128]{1,0:T(8,128)(2,1)} %get-tuple-element.65.q_ref, bf16[6144,256]{1,0:T(8,128)(2,1)} %all-gather.6.cloned.1.call-done.kv_ref), custom_call_target="tpu_custom_call" | custom-call | flops 19327352832 | bytes 3145728 | tf_op jit(solution)/shard_map/attend/pallas_call | solution.py:469
  218.6 0.0 all-to-all-done.2
  218.6 0.0 copy-start
  218.6 5.2 %all-to-all-start.3 = ((bf16[8,192,128]{2,1,0:T(8,128)(2,1)}), bf16[8,192,128]{2,1,0:T(8,128)(2,1)S(1)}, u32[]{:S(2)}, u32[]{:S(2)}) async-start(bf16[8,192,128]{2,1,0:T(8,128)(2,1)} %bitcast.23), calls=%async_computation.3 | async-start | bytes 786432 | tf_op jit(solution)/shard_map/all_to_all | solution.py:574
  223.8 0.0 all-gather.8.cloned.1.call-done.kv_ref
  223.8 14.3 %attend.5 = bf16[1536,128]{1,0:T(8,128)(2,1)} custom-call(bf16[1536,128]{1,0:T(8,128)(2,1)} %get-tuple-element.83.q_ref, bf16[6144,128]{1,0:T(8,128)(2,1)} %all-gather.8.cloned.1.call-done.kv_ref), custom_call_target="tpu_custom_call" | custom-call | flops 9663676416 | bytes 1572864 | tf_op jit(solution)/shard_map/attend/pallas_call | solution.py:469
  238.1 0.0 copy-done
  238.1 0.0 all-to-all-done.3
  238.1 0.0 copy-start.1
  238.1 12.9 %all_to_all.26 = bf16[8,192,128]{2,1,0:T(8,128)(2,1)} all-to-all(bf16[8,192,128]{2,1,0:T(8,128)(2,1)} %bitcast.24), channel_id=1, replica_groups=mesh['dp'=1,'col'=4,'row'=8] {'row'}, dimensions={0} | all-to-all | bytes 786432 | tf_op jit(solution)/shard_map/all_to_all | solution.py:574
  251.0 0.0 copy-done.1
  251.0 7.2 %outproj.1 = (bf16[2,4,48,1280]{3,2,1,0:T(8,128)(2,1)}, bf16[2,4,2,1280]{3,2,1,0:T(2,128)(2,1)}, f32[8,128]{1,0:T(8,128)}) custom-call(bf16[2,4,192,128]{3,2,1,0:T(8,128)(2,1)} %bitcast.18, bf16[2,4,192,128]{3,2,1,0:T(8,128)(2,1)} %bitcast.19, bf16[2,4,192,128]{3,2,1,0:T(8,128)(2,1)} %bitcast.20, bf16[4,20,64,1280]{3,2,1,0:T(8,128)(2,1)} %bitcast.12, ...), custom_call_target="tpu_custom_call" | custom-call | flops 1258291200 | bytes 3276800 | tf_op jit(solution)/shard_map/outproj/pallas_call | solution.py:521
  258.1 10.4 %exchange.8 = (f32[8,128]{1,0:T(8,128)}, bf16[2,48,1280]{2,1,0:T(8,128)(2,1)}, bf16[2,48,1280]{2,1,0:T(8,128)(2,1)}, bf16[2,6,2,1280]{3,2,1,0:T(2,128)(2,1)}) custom-call(f32[8,128]{1,0:T(8,128)} %get-tuple-element.69.refs_0_, bf16[2,4,48,1280]{3,2,1,0:T(8,128)(2,1)} %get-tuple-element.68.refs_1_.x_ref.add_ref, bf16[2,4,2,1280]{3,2,1,0:T(2,128)(2,1)} %get-tuple-element.70.refs_2_), custom_call_target="tpu_custom_call" | custom-call | tf_op jit(solution)/shard_map/exchange/pallas_call | solution.py:179
  268.5 18.9 %conv.6 = (bf16[2,4,48,1280]{3,2,1,0:T(8,128)(2,1)}, bf16[2,4,2,1280]{3,2,1,0:T(2,128)(2,1)}, f32[8,128]{1,0:T(8,128)}) custom-call(bf16[2,4,48,1280]{3,2,1,0:T(8,128)(2,1)} %get-tuple-element.68.refs_1_.x_ref.add_ref, bf16[2,48,1280]{2,1,0:T(8,128)(2,1)} %get-tuple-element.71.top_ref, bf16[2,48,1280]{2,1,0:T(8,128)(2,1)} %get-tuple-element.72.bot_ref, ...), custom_call_target="tpu_custom_call" | custom-call | flops 11324620800 | bytes 29491200 | tf_op jit(solution)/shard_map/conv/pallas_call | solution.py:275
  287.4 10.8 %exchange.9 = (f32[8,128]{1,0:T(8,128)}, bf16[2,48,1280]{2,1,0:T(8,128)(2,1)}, bf16[2,48,1280]{2,1,0:T(8,128)(2,1)}, bf16[2,6,2,1280]{3,2,1,0:T(2,128)(2,1)}) custom-call(f32[8,128]{1,0:T(8,128)} %get-tuple-element.76.refs_0_, bf16[2,4,48,1280]{3,2,1,0:T(8,128)(2,1)} %get-tuple-element.75.refs_1_.x_ref, bf16[2,4,2,1280]{3,2,1,0:T(2,128)(2,1)} %get-tuple-element.77.refs_2_), custom_call_target="tpu_custom_call" | custom-call | tf_op jit(solution)/shard_map/exchange/pallas_call | solution.py:179
  298.2 19.2 %conv.7 = (bf16[2,4,48,1280]{3,2,1,0:T(8,128)(2,1)}, bf16[2,4,2,1280]{3,2,1,0:T(2,128)(2,1)}, f32[8,128]{1,0:T(8,128)}) custom-call(bf16[2,4,48,1280]{3,2,1,0:T(8,128)(2,1)} %get-tuple-element.75.refs_1_.x_ref, bf16[2,48,1280]{2,1,0:T(8,128)(2,1)} %get-tuple-element.78.top_ref, bf16[2,48,1280]{2,1,0:T(8,128)(2,1)} %get-tuple-element.79.bot_ref, ...), custom_call_target="tpu_custom_call" | custom-call | flops 11324620800 | bytes 29491200 | tf_op jit(solution)/shard_map/conv/pallas_call | solution.py:275
Async XLA Ops:
  6.5 147.1 %all-gather.4.cloned.1.call-start = ((), (), s32[]{:S(2)}) async-start(), calls=%async_computation.5 | async-start | bytes 3932160 | tf_op jit(solution)/shard_map/all_gather | solution.py:568
  118.4 29.1 %all-to-all-start.1 = ((bf16[8,192,640]{2,1,0:T(8,128)(2,1)}), bf16[8,192,640]{2,1,0:T(8,128)(2,1)S(1)}, u32[]{:S(2)}, u32[]{:S(2)}) async-start(bf16[8,192,640]{2,1,0:T(8,128)(2,1)} %bitcast.17), calls=%async_computation.1 | async-start | bytes 3932160 | tf_op jit(solution)/shard_map/all_to_all | solution.py:559
  122.8 69.4 %all-gather.6.cloned.1.call-start = ((), (), s32[]{:S(2)}) async-start(), calls=%async_computation.6 | async-start | bytes 3932160 | tf_op jit(solution)/shard_map/all_gather | solution.py:568
  148.6 75.2 %all-gather.8.cloned.1.call-start = ((), (), s32[]{:S(2)}) async-start(), calls=%async_computation.7 | async-start | bytes 1966080 | tf_op jit(solution)/shard_map/all_gather | solution.py:568
  180.0 38.5 %all-to-all-start.2 = ((bf16[8,192,128]{2,1,0:T(8,128)(2,1)}), bf16[8,192,128]{2,1,0:T(8,128)(2,1)S(1)}, u32[]{:S(2)}, u32[]{:S(2)}) async-start(bf16[8,192,128]{2,1,0:T(8,128)(2,1)} %bitcast.22), calls=%async_computation.2 | async-start | bytes 786432 | tf_op jit(solution)/shard_map/all_to_all | solution.py:574
  218.6 19.5 %copy-start = (bf16[8,192,128]{2,1,0:T(8,128)(2,1)}, bf16[8,192,128]{2,1,0:T(8,128)(2,1)S(1)}, u32[]{:S(2)}) copy-start(bf16[8,192,128]{2,1,0:T(8,128)(2,1)S(1)} %all-to-all-done.2) | copy-start | bytes 1179652
  218.6 19.5 %all-to-all-start.3 = ((bf16[8,192,128]{2,1,0:T(8,128)(2,1)}), bf16[8,192,128]{2,1,0:T(8,128)(2,1)S(1)}, u32[]{:S(2)}, u32[]{:S(2)}) async-start(bf16[8,192,128]{2,1,0:T(8,128)(2,1)} %bitcast.23), calls=%async_computation.3 | async-start | bytes 786432 | tf_op jit(solution)/shard_map/all_to_all | solution.py:574
  238.1 12.9 %copy-start.1 = (bf16[8,192,128]{2,1,0:T(8,128)(2,1)}, bf16[8,192,128]{2,1,0:T(8,128)(2,1)S(1)}, u32[]{:S(2)}) copy-start(bf16[8,192,128]{2,1,0:T(8,128)(2,1)S(1)} %all-to-all-done.3) | copy-start | bytes 1179652
Sparse Core Ops, SparseCore 0:
  118.6 35.0 all-gather.3
  155.3 36.9 all-gather.5
  193.8 24.0 all-gather.7
